TPU v7x, 8 devices: a whole 2x2x1 slice. The times are simulated.
8 devices in a mesh: pod: 1 (over z), dp: 2 (over y), stage: 4 (over x, core).
Axes of the slice: x: 2, y: 2, z: 1, core: 2. Of those that a mesh axis runs over, the one named last changes fastest.
Arguments:
- x_emb: bfloat16 [4, 512, 2048], P(None, ('pod', 'dp'))
- labels: int32 [4, 512], P(None, ('pod', 'dp'))
- norm_gain: float32 [4, 1, 2048], P(('pod', 'stage'))
- w_up: bfloat16 [4, 1, 2048, 8192], P(('pod', 'stage'))
- w_down: bfloat16 [4, 1, 8192, 2048], P(('pod', 'stage'))
- w_out: bfloat16 [49152, 2048], P(('pod', 'stage'))
Outputs:
- output 1: float32 [1], P('pod')
- output 2: float32 [4, 512, 2048], P(None, ('pod', 'dp'), 'stage')
- output 3: float32 [4, 1, 2048], P(('pod', 'stage'))
- output 4: float32 [4, 1, 2048, 8192], P(('pod', 'stage'))
- output 5: float32 [4, 1, 8192, 2048], P(('pod', 'stage'))
- output 6: float32 [49152, 2048], P(('pod', 'stage'))
All inputs are finite; a program needn't handle non-finite values.
Results may differ from a plain program's by a relative error of at most 0.02.
Values are sent between devices in bfloat16 or wider.
A program may use at most 1.5 GiB of HBM per device.

v0:
```python
import jax
import jax.numpy as jnp
from jax import lax
from jax.sharding import PartitionSpec as P

NORM_EPS = 1e-6


def norm_apply(h_f32, gain_vec):
    inv_rms = lax.rsqrt(jnp.mean(h_f32 * h_f32, axis=-1, keepdims=True) + NORM_EPS)
    return h_f32 * inv_rms * gain_vec


def block_forward(h_in, gain_vec, w_up, w_down):
    h_f32 = h_in.astype(jnp.float32)
    normed = norm_apply(h_f32, gain_vec).astype(jnp.bfloat16)
    pre_act = jnp.dot(normed, w_up, preferred_element_type=jnp.float32)
    act_bf16 = jax.nn.gelu(pre_act).astype(jnp.bfloat16)
    return (h_f32 + jnp.dot(act_bf16, w_down, preferred_element_type=jnp.float32)).astype(jnp.bfloat16)


def block_backward(h_in, grad_out, gain_vec, w_up, w_down):
    h_f32 = h_in.astype(jnp.float32)
    normed_f, norm_vjp = jax.vjp(norm_apply, h_f32, gain_vec)
    normed = normed_f.astype(jnp.bfloat16)
    pre_act = jnp.dot(normed, w_up, preferred_element_type=jnp.float32)
    act_f, gelu_vjp = jax.vjp(jax.nn.gelu, pre_act)
    act_bf16 = act_f.astype(jnp.bfloat16)
    d_down = jnp.einsum('tf,td->fd', act_bf16, grad_out, preferred_element_type=jnp.float32)
    d_act = jnp.einsum('td,fd->tf', grad_out, w_down, preferred_element_type=jnp.float32)
    d_pre = gelu_vjp(d_act)[0].astype(jnp.bfloat16)
    d_up = jnp.einsum('td,tf->df', normed, d_pre, preferred_element_type=jnp.float32)
    d_normed = jnp.einsum('tf,df->td', d_pre, w_up, preferred_element_type=jnp.float32)
    d_h, d_gain = norm_vjp(d_normed)
    return grad_out.astype(jnp.float32) + d_h, d_gain, d_up, d_down


def stage_forward(h_in, gain_stack, up_stack, down_stack):
    layer_inputs = []
    for layer_id in range(gain_stack.shape[0]):
        layer_inputs.append(h_in)
        h_in = block_forward(h_in, gain_stack[layer_id], up_stack[layer_id], down_stack[layer_id])
    return h_in, jnp.stack(layer_inputs)


def stage_backward(layer_inputs, grad_out, gain_stack, up_stack, down_stack):
    d_gains, d_ups, d_downs = [], [], []
    grad_f = grad_out.astype(jnp.float32)
    for layer_id in reversed(range(gain_stack.shape[0])):
        grad_f, d_gain, d_up, d_down = block_backward(layer_inputs[layer_id], grad_out, gain_stack[layer_id], up_stack[layer_id], down_stack[layer_id])
        grad_out = grad_f.astype(jnp.bfloat16)
        d_gains.append(d_gain)
        d_ups.append(d_up)
        d_downs.append(d_down)
    return grad_f, jnp.stack(d_gains[::-1]), jnp.stack(d_ups[::-1]), jnp.stack(d_downs[::-1])


def solution(mesh):
    n_stage = mesh.shape['stage']
    n_dp = mesh.shape['dp']
    fwd_perm = [(src_id, src_id + 1) for src_id in range(n_stage - 1)]
    bwd_perm = [(src_id + 1, src_id) for src_id in range(n_stage - 1)]

    def device_step(x_emb, labels, norm_gain, w_up, w_down, w_out):
        n_micro, n_tok, d_model = x_emb.shape
        gain_stack, up_stack, down_stack = norm_gain[0], w_up[0], w_down[0]
        n_layer = gain_stack.shape[0]
        vocab_loc = w_out.shape[0]
        stage_id = lax.axis_index('stage')
        is_last = stage_id == n_stage - 1
        tick_ids = jnp.arange(n_micro + n_stage - 1)
        loss_scale = 1.0 / (n_micro * n_tok * n_dp)

        def fwd_tick(state_in, tick_id):
            recv_buf, saved_in, finals = state_in
            micro_id = tick_id - stage_id
            is_valid = (micro_id >= 0) & (micro_id < n_micro)
            slot_id = jnp.clip(micro_id, 0, n_micro - 1)
            first_in = lax.dynamic_index_in_dim(x_emb, slot_id, 0, keepdims=False)
            h_in = jnp.where(stage_id == 0, first_in, recv_buf)
            h_out, layer_inputs = stage_forward(h_in, gain_stack, up_stack, down_stack)
            prev_in = lax.dynamic_index_in_dim(saved_in, slot_id, 0, keepdims=False)
            saved_in = lax.dynamic_update_index_in_dim(saved_in, jnp.where(is_valid, layer_inputs, prev_in), slot_id, 0)
            prev_out = lax.dynamic_index_in_dim(finals, slot_id, 0, keepdims=False)
            finals = lax.dynamic_update_index_in_dim(finals, jnp.where(is_valid, h_out, prev_out), slot_id, 0)
            recv_buf = lax.ppermute(h_out, 'stage', fwd_perm)
            return (recv_buf, saved_in, finals), None

        init_fwd = (jnp.zeros((n_tok, d_model), jnp.bfloat16), jnp.zeros((n_micro, n_layer, n_tok, d_model), jnp.bfloat16), jnp.zeros((n_micro, n_tok, d_model), jnp.bfloat16))
        fwd_state, fwd_ys = lax.scan(fwd_tick, init_fwd, tick_ids)
        saved_in, finals = fwd_state[1], fwd_state[2]
        h_final = lax.psum(jnp.where(is_last, finals, jnp.zeros_like(finals)), 'stage')
        col_ids = stage_id * vocab_loc + lax.broadcasted_iota(jnp.int32, (1, vocab_loc), 1)

        def head_micro(state_in, batch_in):
            loss_sum, acc_out = state_in
            h_mb, lab_mb = batch_in
            logits = jnp.einsum('td,vd->tv', h_mb, w_out, preferred_element_type=jnp.float32)
            row_max = lax.pmax(jnp.max(logits, axis=-1), 'stage')
            is_label = col_ids == lab_mb[:, None]
            local_stats = jnp.stack([jnp.sum(jnp.exp(logits - row_max[:, None]), axis=-1), jnp.sum(jnp.where(is_label, logits, 0.0), axis=-1)])
            total_stats = lax.psum(local_stats, 'stage')
            log_norm = row_max + jnp.log(total_stats[0])
            softmax_p = jnp.exp(logits - log_norm[:, None])
            d_logits = ((softmax_p - is_label.astype(jnp.float32)) * loss_scale).astype(jnp.bfloat16)
            d_hid = jnp.einsum('tv,vd->td', d_logits, w_out, preferred_element_type=jnp.float32)
            acc_out = acc_out + jnp.einsum('tv,td->vd', d_logits, h_mb, preferred_element_type=jnp.float32)
            return (loss_sum + jnp.sum(log_norm - total_stats[1]), acc_out), d_hid

        head_state, d_hid = lax.scan(head_micro, (jnp.zeros((), jnp.float32), jnp.zeros((vocab_loc, d_model), jnp.float32)), (h_final, labels))
        loss_sum, acc_out = head_state
        d_top = lax.psum(d_hid, 'stage').astype(jnp.bfloat16)

        def bwd_tick(state_in, tick_id):
            recv_buf, acc_gain, acc_up, acc_down, grad_first = state_in
            micro_id = tick_id - (n_stage - 1 - stage_id)
            is_valid = (micro_id >= 0) & (micro_id < n_micro)
            slot_id = jnp.clip(micro_id, 0, n_micro - 1)
            top_in = lax.dynamic_index_in_dim(d_top, slot_id, 0, keepdims=False)
            grad_in = jnp.where(is_last, top_in, recv_buf)
            layer_inputs = lax.dynamic_index_in_dim(saved_in, slot_id, 0, keepdims=False)
            grad_f, d_gain, d_up, d_down = stage_backward(layer_inputs, grad_in, gain_stack, up_stack, down_stack)
            acc_gain = jnp.where(is_valid, acc_gain + d_gain, acc_gain)
            acc_up = jnp.where(is_valid, acc_up + d_up, acc_up)
            acc_down = jnp.where(is_valid, acc_down + d_down, acc_down)
            prev_grad = lax.dynamic_index_in_dim(grad_first, slot_id, 0, keepdims=False)
            grad_first = lax.dynamic_update_index_in_dim(grad_first, jnp.where(is_valid, grad_f, prev_grad), slot_id, 0)
            recv_buf = lax.ppermute(grad_f.astype(jnp.bfloat16), 'stage', bwd_perm)
            return (recv_buf, acc_gain, acc_up, acc_down, grad_first), None

        init_bwd = (jnp.zeros((n_tok, d_model), jnp.bfloat16), jnp.zeros(gain_stack.shape, jnp.float32), jnp.zeros(up_stack.shape, jnp.float32), jnp.zeros(down_stack.shape, jnp.float32), jnp.zeros((n_micro, n_tok, d_model), jnp.float32))
        bwd_state, bwd_ys = lax.scan(bwd_tick, init_bwd, tick_ids)
        grad_first = bwd_state[4]
        grad_x = lax.psum_scatter(jnp.where(stage_id == 0, grad_first, jnp.zeros_like(grad_first)), 'stage', scatter_dimension=2, tiled=True)
        acc_gain, acc_up, acc_down, acc_out = lax.psum((bwd_state[1], bwd_state[2], bwd_state[3], acc_out), 'dp')
        loss_mean = lax.psum(loss_sum, 'dp') * loss_scale
        return loss_mean.reshape(1), grad_x, acc_gain[None], acc_up[None], acc_down[None], acc_out

    tok_spec = ('pod', 'dp')
    stage_spec = ('pod', 'stage')
    in_specs = (P(None, tok_spec, None), P(None, tok_spec), P(stage_spec, None, None), P(stage_spec, None, None, None), P(stage_spec, None, None, None), P(stage_spec, None))
    out_specs = (P('pod'), P(None, tok_spec, 'stage'), P(stage_spec, None, None), P(stage_spec, None, None, None), P(stage_spec, None, None, None), P(stage_spec, None))
    return jax.shard_map(device_step, mesh=mesh, in_specs=in_specs, out_specs=out_specs, check_vma=False)
```

profile of v0, /device:TPU:0, one launch (start us, length us, event | category | flops | bytes accessed | tf_op | source)
XLA Modules:
  0.0 7607.0 jit_solution(1694745487744415157)
XLA Ops:
  12.4 350.5 %while.51 = (s32[]{:T(128)}, bf16[256,2048]{1,0:T(8,128)(2,1)S(1)}, bf16[4,1,256,2048]{3,2,1,0:T(8,128)(2,1)}, bf16[4,256,2048]{2,1,0:T(8,128)(2,1)}, pred[]{:T(...) while((s32[]{:T(128)}, bf16[256,2048]{1,0:T(8,128)(2,1)S(1)}, ...), condition=%wide.region_2.3_spmd, body=%wide.region_0.2_spmd.sunk | while | flops 17205559296 | bytes 87044880 | solution.py:90
  20.5 27.5 bitcast_dynamic-update-slice_fusion.7
  61.0 27.5 bitcast_dynamic-update-slice_fusion.7
  112.8 27.5 bitcast_dynamic-update-slice_fusion.7
  164.4 27.5 bitcast_dynamic-update-slice_fusion.7
  216.1 27.5 bitcast_dynamic-update-slice_fusion.7
  267.7 27.5 bitcast_dynamic-update-slice_fusion.7
  319.3 27.5 bitcast_dynamic-update-slice_fusion.7
  365.4 93.5 %all-reduce.7.cloned.1.call-done = bf16[4,256,2048]{2,1,0:T(8,128)(2,1)} async-done(((bf16[4,256,2048]{2,1,0:T(8,128)(2,1)}), bf16[4,256,2048]{2,1,0:T(8,128)(2,1)}) %all-reduce.7.cloned.1.call-update) | async-done | bytes 4194320 | tf_op jit(solution)/shard_map/psum | solution.py:92
  463.1 525.3 %while.52 = (s32[]{:T(128)}, f32[]{:T(128)}, f32[12288,2048]{1,0:T(8,128)}, f32[4,256,2048]{2,1,0:T(8,128)}, bf16[4,256,2048]{2,1,0:T(8,128)(2,1)}, /*index=5*/b...) while((s32[]{:T(128)}, f32[]{:T(128)}, ...), condition=%wide.region_11.12_spmd.clone, body=%wide.region_4.11_spmd.clone.sunk | while | flops 38761672704 | bytes 356742272 | solution.py:110
  463.8 24.1 fusion.162
  507.4 25.2 fusion.163
  532.7 37.9 select_add_fusion.2
  571.3 24.1 fusion.162
  615.5 25.2 fusion.163
  640.6 69.3 select_add_fusion.2
  710.7 24.1 fusion.162
  755.1 25.2 fusion.163
  780.4 69.3 select_add_fusion.2
  850.4 24.1 fusion.162
  893.9 25.2 fusion.163
  919.1 69.3 select_add_fusion.2
  988.4 146.3 %all-reduce.14 = bf16[4,256,2048]{2,1,0:T(8,128)(2,1)} all-reduce(f32[4,256,2048]{2,1,0:T(8,128)} %get-tuple-element.328), channel_id=1, replica_groups=mesh['pod'=1,'dp'=2,'stage'=4] {'stage'}, use_global_device_ids=true, to_apply=%region_13.14 | all-reduce | flops 2097152 | bytes 12582912 | tf_op jit(solution)/shard_map/psum | solution.py:112
  1140.5 1138.7 %while.53 = (s32[]{:T(128)}, bf16[256,2048]{1,0:T(8,128)(2,1)}, f32[1,2048]{1,0:T(1,128)}, f32[1,2048,8192]{2,1,0:T(8,128)}, f32[1,8192,2048]{2,1,0:T(8,128)}, /...) while((s32[]{:T(128)}, bf16[256,2048]{1,0:T(8,128)(2,1)}, ...), condition=%wide.region_18.19_spmd.clone, body=%wide.region_14.18_spmd.clone.sunk | while | flops 43130560512 | bytes 440555904 | solution.py:132
  1145.8 17.4 fusion.174
  1163.2 20.6 fusion.175
  1207.6 26.4 add_select_fusion.5
  1234.0 25.4 add_select_fusion.4
  1268.5 17.4 fusion.174
  1285.9 20.6 fusion.175
  1330.3 49.7 add_select_fusion.5
  1380.1 48.6 add_select_fusion.4
  1437.9 17.4 fusion.174
  1455.3 20.6 fusion.175
  1475.8 16.4 fusion.176
  1499.7 49.7 add_select_fusion.5
  1549.4 48.6 add_select_fusion.4
  1607.2 17.4 fusion.174
  1624.6 20.6 fusion.175
  1645.2 16.4 fusion.176
  1669.0 49.7 add_select_fusion.5
  1718.7 48.6 add_select_fusion.4
  1776.5 17.4 fusion.174
  1793.9 20.6 fusion.175
  1814.5 16.4 fusion.176
  1838.3 49.7 add_select_fusion.5
  1888.1 48.6 add_select_fusion.4
  1945.8 17.4 fusion.174
  1963.2 20.6 fusion.175
  1983.7 16.4 fusion.176
  2007.6 49.7 add_select_fusion.5
  2057.3 48.6 add_select_fusion.4
  2115.0 17.4 fusion.174
  2132.5 20.6 fusion.175
  2153.0 16.4 fusion.176
  2176.8 49.7 add_select_fusion.5
  2226.6 48.6 add_select_fusion.4
  2296.5 60.1 reduce-scatter.2.cloned.1.call-done
  2356.6 1454.5 %all-reduce.11.cloned.1.call-done = f32[1,1,8192,2048]{3,2,1,0:T(8,128)} async-done(((f32[1,1,8192,2048]{3,2,1,0:T(8,128)}), f32[1,1,8192,2048]{3,2,1,0:T(8,128)}) %all-reduce.11.cloned.1.call-update) | async-done | bytes 67108880 | tf_op jit(solution)/shard_map/psum | solution.py:135
  3811.1 1456.6 %all-reduce.9.cloned.1.call-done = f32[1,1,2048,8192]{3,2,1,0:T(8,128)} async-done(((f32[1,1,2048,8192]{3,2,1,0:T(8,128)}), f32[1,1,2048,8192]{3,2,1,0:T(8,128)}) %all-reduce.9.cloned.1.call-update) | async-done | bytes 67108880 | tf_op jit(solution)/shard_map/psum | solution.py:135
  5267.7 2179.2 %all-reduce.13.cloned.1.call-done = f32[12288,2048]{1,0:T(8,128)} async-done(((f32[12288,2048]{1,0:T(8,128)}), f32[12288,2048]{1,0:T(8,128)}) %all-reduce.13.cloned.1.call-update) | async-done | bytes 100663312 | tf_op jit(solution)/shard_map/psum | solution.py:135
  7446.9 43.9 copy.66
  7490.8 43.6 copy.67
  7534.4 64.5 copy.68
  (226 shorter events, 410.6 us)
Async XLA Ops:
  7.2 5.2 copy-start
  7.2 451.7 %all-reduce.7.cloned.1.call-start = ((), (), s32[]{:S(2)}) async-start(), calls=%async_computation.1 | async-start | bytes 8388608 | tf_op jit(solution)/shard_map/psum | solution.py:92
  48.0 5.0 collective-permute-start
  88.5 16.3 collective-permute-start
  140.3 16.1 collective-permute-start
  191.9 16.2 collective-permute-start
  243.6 16.1 collective-permute-start
  295.2 16.1 collective-permute-start
  346.8 16.1 collective-permute-start
  365.1 1991.5 %reduce-scatter.2.cloned.1.call-start = ((), (), s32[]{:S(2)}) async-start(), calls=%async_computation.2 | async-start | bytes 10485760 | tf_op jit(solution)/shard_map/reduce_scatter | solution.py:134
  988.4 152.2 %copy-start.1 = (f32[1,1,2048]{2,1,0:T(1,128)S(1)}, f32[1,1,2048]{2,1,0:T(1,128)}, u32[]{:S(2)}) copy-start(f32[1,1,2048]{2,1,0:T(1,128)} %param.14) | copy-start | bytes 24580
  1203.2 60.3 collective-permute-start.1
  1234.0 25.4 copy-start.2
  1259.4 4.0 copy-start.3
  1325.9 106.9 %collective-permute-start.1 = (bf16[256,2048]{1,0:T(8,128)(2,1)}, bf16[256,2048]{1,0:T(8,128)(2,1)}, u32[]{:S(2)}, u32[]{:S(2)}) collective-permute-start(bf16[256,2048]{1,0:T(8,128)(2,1)} %fusion.177), channel_id=1, source_target_pairs={{1,0},{2,1},{3,2},{5,4},{6,5},{7,6}} | collective-permute-start | bytes 3145736 | tf_op jit(solution)/shard_map/while/body/eval_jaxpr/ppermute | solution.py:128
  1380.1 48.6 copy-start.2
  1428.7 4.0 copy-start.3
  1495.2 106.9 %collective-permute-start.1 = (bf16[256,2048]{1,0:T(8,128)(2,1)}, bf16[256,2048]{1,0:T(8,128)(2,1)}, u32[]{:S(2)}, u32[]{:S(2)}) collective-permute-start(bf16[256,2048]{1,0:T(8,128)(2,1)} %fusion.177), channel_id=1, source_target_pairs={{1,0},{2,1},{3,2},{5,4},{6,5},{7,6}} | collective-permute-start | bytes 3145736 | tf_op jit(solution)/shard_map/while/body/eval_jaxpr/ppermute | solution.py:128
  1549.4 48.6 copy-start.2
  1598.1 4.0 copy-start.3
  1664.5 106.9 %collective-permute-start.1 = (bf16[256,2048]{1,0:T(8,128)(2,1)}, bf16[256,2048]{1,0:T(8,128)(2,1)}, u32[]{:S(2)}, u32[]{:S(2)}) collective-permute-start(bf16[256,2048]{1,0:T(8,128)(2,1)} %fusion.177), channel_id=1, source_target_pairs={{1,0},{2,1},{3,2},{5,4},{6,5},{7,6}} | collective-permute-start | bytes 3145736 | tf_op jit(solution)/shard_map/while/body/eval_jaxpr/ppermute | solution.py:128
  1718.7 48.6 copy-start.2
  1767.4 4.0 copy-start.3
  1833.9 106.8 %collective-permute-start.1 = (bf16[256,2048]{1,0:T(8,128)(2,1)}, bf16[256,2048]{1,0:T(8,128)(2,1)}, u32[]{:S(2)}, u32[]{:S(2)}) collective-permute-start(bf16[256,2048]{1,0:T(8,128)(2,1)} %fusion.177), channel_id=1, source_target_pairs={{1,0},{2,1},{3,2},{5,4},{6,5},{7,6}} | collective-permute-start | bytes 3145736 | tf_op jit(solution)/shard_map/while/body/eval_jaxpr/ppermute | solution.py:128
  1888.1 48.6 copy-start.2
  1936.7 4.0 copy-start.3
  2003.1 106.9 %collective-permute-start.1 = (bf16[256,2048]{1,0:T(8,128)(2,1)}, bf16[256,2048]{1,0:T(8,128)(2,1)}, u32[]{:S(2)}, u32[]{:S(2)}) collective-permute-start(bf16[256,2048]{1,0:T(8,128)(2,1)} %fusion.177), channel_id=1, source_target_pairs={{1,0},{2,1},{3,2},{5,4},{6,5},{7,6}} | collective-permute-start | bytes 3145736 | tf_op jit(solution)/shard_map/while/body/eval_jaxpr/ppermute | solution.py:128
  2057.3 48.6 copy-start.2
  2105.9 4.0 copy-start.3
  2172.4 106.8 %collective-permute-start.1 = (bf16[256,2048]{1,0:T(8,128)(2,1)}, bf16[256,2048]{1,0:T(8,128)(2,1)}, u32[]{:S(2)}, u32[]{:S(2)}) collective-permute-start(bf16[256,2048]{1,0:T(8,128)(2,1)} %fusion.177), channel_id=1, source_target_pairs={{1,0},{2,1},{3,2},{5,4},{6,5},{7,6}} | collective-permute-start | bytes 3145736 | tf_op jit(solution)/shard_map/while/body/eval_jaxpr/ppermute | solution.py:128
  2226.6 48.6 copy-start.2
  2275.2 4.0 copy-start.3
  2287.6 1523.5 %all-reduce.11.cloned.1.call-start = ((), (), s32[]{:S(2)}) async-start(), calls=%async_computation.4 | async-start | bytes 134217728 | tf_op jit(solution)/shard_map/psum | solution.py:135
  2288.3 2979.4 %all-reduce.9.cloned.1.call-start = ((), (), s32[]{:S(2)}) async-start(), calls=%async_computation.3 | async-start | bytes 134217728 | tf_op jit(solution)/shard_map/psum | solution.py:135
  2288.9 5158.0 %all-reduce.13.cloned.1.call-start = ((), (), s32[]{:S(2)}) async-start(), calls=%async_computation.5 | async-start | bytes 201326592 | tf_op jit(solution)/shard_map/psum | solution.py:135
  2288.9 0.7 copy-start.4
Sparse Core Ops, SparseCore 0:
  365.2 93.5 all-reduce.6
  2287.7 68.8 reduce-scatter.1
  2359.6 1451.4 all-reduce.10
  3814.0 1453.6 all-reduce.8
  5270.6 2176.3 all-reduce.12
where the time goes:
time: 7620 us; the launch traced here: 7610 us
  waiting for transfers between devices  5260 us (69%)
  matrix products  1660 us (22%)
  local copies, waits for them, and re-layouts  230 us (3%)
  blocking collectives  200 us (3%)
  other arithmetic  133 us (2%)
  starting transfers between devices  95.8 us (1%)
    psum x3, waiting for transfers between devices, device_step(): lax.psum((bwd_state[1], bwd_state[2], bwd_state[3], acc_out), 'dp')  5090 us
    dot_general x7, matrix products, block_backward(): jnp.einsum('tf,td->fd', act_bf16, grad_out, preferred_element_type=jnp.fl...  325 us
    dot_general x7, matrix products, block_backward(): jnp.einsum('td,tf->df', normed, d_pre, preferred_element_type=jnp.float32)  317 us
    dot_general x4, matrix products, head_micro(): jnp.einsum('tv,td->vd', d_logits, h_mb, preferred_element_type=jnp.float32)  246 us
    dot_general x7, matrix products, block_forward(): jnp.dot(act_bf16, w_down, preferred_element_type=jnp.float32)  193 us
  transfers between devices with their start and end apart: 19, of which 12 were waited for; matrix products, arithmetic and copies ran while one was open for 9% of the time, Pallas kernels for 0%

commit v1 on v0

v1 whole, which is shorter than its diff:
```python
import functools

import jax
import jax.numpy as jnp
from jax import lax
from jax.experimental import pallas as pl
from jax.experimental.pallas import tpu as pltpu
from jax.sharding import PartitionSpec as P

NORM_EPS = 1e-6
FB = 1024
WB = 256
VB = 512
RING = 3
GELU_C = 0.7978845608028654
GELU_K = 0.044715
VMEM_LIMIT = 67_000_000
MESH = pl.DeviceIdType.MESH
F32 = jnp.float32
BF16 = jnp.bfloat16
ANY = pl.BlockSpec(memory_space=pl.ANY)


def dot_nn(a, b):
    return jnp.dot(a, b, preferred_element_type=F32)


def dot_nt(a, b):
    return lax.dot_general(a, b, (((1,), (1,)), ((), ())), preferred_element_type=F32)


def dot_tn(a, b):
    return lax.dot_general(a, b, (((0,), (0,)), ((), ())), preferred_element_type=F32)


def gelu_and_slope(a):
    sq = a * a
    t = jnp.tanh(a * (GELU_C + (GELU_C * GELU_K) * sq))
    cdf = 0.5 + 0.5 * t
    slope = cdf + a * ((0.5 - 0.5 * (t * t)) * (GELU_C + (3.0 * GELU_C * GELU_K) * sq))
    return a * cdf, slope


def params(collective_id=None, **more):
    return pltpu.CompilerParams(
        vmem_limit_bytes=VMEM_LIMIT,
        collective_id=collective_id,
        has_side_effects=collective_id is not None,
        **more,
    )


def cost(flops, bytes_accessed):
    return pl.CostEstimate(flops=int(flops), bytes_accessed=int(bytes_accessed), transcendentals=0)


def fwd_kernel(n_stage, n_micro, n_tile, x_ref, g_ref, w1_ref, w2_ref, hin_ref, hinp_ref, hfin_ref, gp_ref, u_ref,
               recv, obuf, norm, acc, w1b, w2b, gpb, ub,
               x_sem, w1_sem, w2_sem, gp_sem, u_sem, hs_sem, fin_sem, send_sem, recv_sem, psend_sem, precv_sem, bsend_sem, frecv_sem):
    stage = lax.axis_index('stage')
    dp = lax.axis_index('dp')
    last = n_stage - 1
    n_rows = recv.shape[1]

    barrier = pltpu.get_barrier_semaphore()
    for step in range(1, n_stage):
        pl.semaphore_signal(barrier, inc=1, device_id={'stage': lax.rem(stage + step, n_stage)}, device_id_type=MESH)
    pl.semaphore_signal(barrier, inc=1, device_id={'dp': 1 - dp}, device_id_type=MESH)

    def x_copy(m):
        return pltpu.make_async_copy(x_ref.at[m], recv.at[m], x_sem.at[m])

    def w1_copy(j):
        return pltpu.make_async_copy(w1_ref.at[:, pl.ds(pl.multiple_of(j * FB, FB), FB)], w1b.at[j], w1_sem.at[j])

    def w2_copy(q):
        slot = lax.rem(q, RING)
        j = lax.rem(q, n_tile)
        return pltpu.make_async_copy(w2_ref.at[pl.ds(pl.multiple_of(j * FB, FB), FB), :], w2b.at[slot], w2_sem.at[slot])

    def gp_copy(m, j, slot):
        return pltpu.make_async_copy(gpb.at[slot], gp_ref.at[m, j], gp_sem.at[slot])

    def u_copy(m, j, slot):
        return pltpu.make_async_copy(ub.at[slot], u_ref.at[j, m], u_sem.at[slot])

    def save_copy(m):
        return pltpu.make_async_copy(recv.at[m], hin_ref.at[m], hs_sem.at[m])

    def peer_copy(m):
        return pltpu.make_async_remote_copy(recv.at[m], hinp_ref.at[m], psend_sem.at[m], precv_sem.at[m],
                                            device_id={'dp': 1 - dp}, device_id_type=MESH)

    def next_copy(m):
        return pltpu.make_async_remote_copy(obuf.at[m], recv.at[m], send_sem.at[m], recv_sem.at[m],
                                            device_id={'stage': lax.rem(stage + 1, n_stage)}, device_id_type=MESH)

    def fin_copy(m):
        return pltpu.make_async_copy(obuf.at[m], hfin_ref.at[m], fin_sem.at[m])

    def bcast_copy(m, k):
        return pltpu.make_async_remote_copy(obuf.at[m], hfin_ref.at[m], bsend_sem.at[m, k], frecv_sem.at[m],
                                            device_id={'stage': k}, device_id_type=MESH)

    w1_copy(0).start()
    w2_copy(0).start()

    @pl.when(stage == 0)
    def _():
        for m in range(n_micro):
            x_copy(m).start()

    for j in range(1, n_tile):
        w1_copy(j).start()
    w2_copy(1).start()

    pl.semaphore_wait(barrier, n_stage)

    def front(m, j):
        q = m * n_tile + j
        slot = lax.rem(q, 2)

        @pl.when(m == 0)
        def _():
            w1_copy(j).wait()

        @pl.when(q >= 2)
        def _():
            gp_copy(m, j, slot).wait()
            u_copy(m, j, slot).wait()

    def micro(m, _):
        @pl.when(stage == 0)
        def _():
            x_copy(m).wait()

        @pl.when(stage > 0)
        def _():
            next_copy(m).wait_recv()

        save_copy(m).start()
        peer_copy(m).start()

        def norm_rows(i, _):
            rows = pl.ds(pl.multiple_of(i * 32, 32), 32)
            r = recv[m, rows, :].astype(F32)
            inv = lax.rsqrt(jnp.mean(r * r, axis=-1, keepdims=True) + NORM_EPS)
            norm[rows, :] = (r * inv * g_ref[...]).astype(BF16)
            return 0

        lax.fori_loop(0, n_rows // 32, norm_rows, 0)

        front(m, 0)
        q0 = m * n_tile
        s0 = lax.rem(q0, 2)
        u, slope = gelu_and_slope(dot_nn(norm[...], w1b[0]))
        gpb[s0] = slope
        ub[s0] = u.astype(BF16)
        gp_copy(m, 0, s0).start()
        u_copy(m, 0, s0).start()
        acc[...] = recv[m].astype(F32)

        def tile(j, _):
            front(m, j)
            q = m * n_tile + j
            slot = lax.rem(q, 2)
            prev = lax.rem(q + 1, 2)
            w2_copy(q - 1).wait()

            @pl.when(q + 1 < n_micro * n_tile)
            def _():
                w2_copy(q + 1).start()

            ring = lax.rem(q - 1, RING)
            acc[...] += dot_nn(ub[prev], w2b[ring])
            u, slope = gelu_and_slope(dot_nn(norm[...], w1b[j]))
            gpb[slot] = slope
            ub[slot] = u.astype(BF16)
            gp_copy(m, j, slot).start()
            u_copy(m, j, slot).start()
            return 0

        lax.fori_loop(1, n_tile, tile, 0)

        q = m * n_tile + n_tile - 1
        w2_copy(q).wait()

        @pl.when(m < n_micro - 1)
        def _():
            w2_copy(q + 2).start()

        obuf[m] = (acc[...] + dot_nn(ub[lax.rem(q, 2)], w2b[lax.rem(q, RING)])).astype(BF16)

        @pl.when(stage < last)
        def _():
            next_copy(m).start()

        @pl.when(stage == last)
        def _():
            fin_copy(m).start()
            for k in range(last):
                bcast_copy(m, k).start()

        return 0

    lax.fori_loop(0, n_micro, micro, 0)

    end = n_micro * n_tile
    for q in (end - 2, end - 1):
        gp_copy(q // n_tile, q % n_tile, q % 2).wait()
        u_copy(q // n_tile, q % n_tile, q % 2).wait()
    for m in range(n_micro):
        save_copy(m).wait()
        peer_copy(m).wait()

        @pl.when(stage < last)
        def _():
            next_copy(m).wait_send()
            bcast_copy(m, 0).wait_recv()

        @pl.when(stage == last)
        def _():
            fin_copy(m).wait()
            for k in range(last):
                bcast_copy(m, k).wait_send()


def forward(n_stage, x, gain, w1, w2):
    n_micro, n_tok, d = x.shape
    f = w1.shape[1]
    n_tile = f // FB
    dma = pltpu.SemaphoreType.DMA
    act = jax.ShapeDtypeStruct(x.shape, BF16)
    return pl.pallas_call(
        functools.partial(fwd_kernel, n_stage, n_micro, n_tile),
        out_shape=(act, act, act,
                   jax.ShapeDtypeStruct((n_micro, n_tile, n_tok, FB), F32),
                   jax.ShapeDtypeStruct((n_tile, n_micro, n_tok, FB), BF16)),
        in_specs=[ANY, pl.BlockSpec(memory_space=pltpu.VMEM), ANY, ANY],
        out_specs=(ANY,) * 5,
        scratch_shapes=[
            pltpu.VMEM((n_micro, n_tok, d), BF16),
            pltpu.VMEM((n_micro, n_tok, d), BF16),
            pltpu.VMEM((n_tok, d), BF16),
            pltpu.VMEM((n_tok, d), F32),
            pltpu.VMEM((n_tile, d, FB), BF16),
            pltpu.VMEM((RING, FB, d), BF16),
            pltpu.VMEM((2, n_tok, FB), F32),
            pltpu.VMEM((2, n_tok, FB), BF16),
            dma((n_micro,)), dma((n_tile,)), dma((RING,)), dma((2,)), dma((2,)), dma((n_micro,)), dma((n_micro,)),
            dma((n_micro,)), dma((n_micro,)), dma((n_micro,)), dma((n_micro,)), dma((n_micro, n_stage - 1)), dma((n_micro,)),
        ],
        compiler_params=params(0),
        cost_estimate=cost(4 * n_micro * n_tok * d * f, 4 * d * f * (1 + n_micro)),
        name='forward',
    )(x, gain, w1, w2)


def bwd_kernel(n_stage, n_micro, n_tile, top_ref, hin_ref, g_ref, w1_ref, w2_ref, gp_ref, dyin_ref, dyp_ref, da_ref, gx_ref, dg_ref,
               recv, obuf, hbuf, acc, xbuf, w1b, w2b, gpb, dab,
               t_sem, w1_sem, w2_sem, gp_sem, da_sem, h_sem, hs_sem, x_sem, send_sem, recv_sem, psend_sem, precv_sem):
    stage = lax.axis_index('stage')
    dp = lax.axis_index('dp')
    last = n_stage - 1
    n_rows = recv.shape[1]
    total = n_micro * n_tile

    barrier = pltpu.get_barrier_semaphore()
    pl.semaphore_signal(barrier, inc=1, device_id={'dp': 1 - dp}, device_id_type=MESH)

    @pl.when(stage > 0)
    def _():
        pl.semaphore_signal(barrier, inc=1, device_id={'stage': stage - 1}, device_id_type=MESH)

    @pl.when(stage < last)
    def _():
        pl.semaphore_signal(barrier, inc=1, device_id={'stage': stage + 1}, device_id_type=MESH)

    def top_copy(m):
        return pltpu.make_async_copy(top_ref.at[m], recv.at[m], t_sem.at[m])

    def w2_copy(j):
        return pltpu.make_async_copy(w2_ref.at[pl.ds(pl.multiple_of(j * FB, FB), FB), :], w2b.at[j], w2_sem.at[j])

    def w1_copy(q):
        slot = lax.rem(q, RING)
        j = lax.rem(q, n_tile)
        return pltpu.make_async_copy(w1_ref.at[:, pl.ds(pl.multiple_of(j * FB, FB), FB)], w1b.at[slot], w1_sem.at[slot])

    def gp_copy(q):
        slot = lax.rem(q, 2)
        return pltpu.make_async_copy(gp_ref.at[lax.div(q, n_tile), lax.rem(q, n_tile)], gpb.at[slot], gp_sem.at[slot])

    def da_copy(m, j, slot):
        return pltpu.make_async_copy(dab.at[slot], da_ref.at[j, m], da_sem.at[slot])

    def h_copy(m):
        return pltpu.make_async_copy(hin_ref.at[m], hbuf, h_sem)

    def save_copy(m):
        return pltpu.make_async_copy(recv.at[m], dyin_ref.at[m], hs_sem.at[m])

    def peer_copy(m):
        return pltpu.make_async_remote_copy(recv.at[m], dyp_ref.at[m], psend_sem.at[m], precv_sem.at[m],
                                            device_id={'dp': 1 - dp}, device_id_type=MESH)

    def next_copy(m):
        slot = lax.rem(m, 2)
        return pltpu.make_async_remote_copy(obuf.at[slot], recv.at[m], send_sem.at[slot], recv_sem.at[m],
                                            device_id={'stage': lax.rem(stage + last, n_stage)}, device_id_type=MESH)

    def x_copy(m):
        return pltpu.make_async_copy(xbuf, gx_ref.at[m], x_sem)

    @pl.when(stage == last)
    def _():
        for m in range(n_micro):
            top_copy(m).start()

    gp_copy(0).start()
    w2_copy(0).start()
    w1_copy(0).start()
    gp_copy(1).start()
    for j in range(1, n_tile):
        w2_copy(j).start()
    w1_copy(1).start()
    dg_ref[...] = jnp.zeros_like(dg_ref)

    def front(m, j):
        q = m * n_tile + j
        slot = lax.rem(q, 2)

        @pl.when(m == 0)
        def _():
            w2_copy(j).wait()

        @pl.when(q >= 2)
        def _():
            da_copy(m, j, slot).wait()

        gp_copy(q).wait()

    def micro(m, _):
        @pl.when(stage == last)
        def _():
            top_copy(m).wait()

        @pl.when(stage < last)
        def _():
            next_copy(m).wait_recv()

        save_copy(m).start()
        h_copy(m).start()

        front(m, 0)
        q0 = m * n_tile
        s0 = lax.rem(q0, 2)
        dab[s0] = (gpb[s0] * dot_nt(recv[m], w2b[0])).astype(BF16)
        da_copy(m, 0, s0).start()
        gp_copy(q0 + 2).start()
        acc[...] = jnp.zeros_like(acc)

        def tile(j, _):
            front(m, j)
            q = m * n_tile + j
            slot = lax.rem(q, 2)
            prev = lax.rem(q + 1, 2)
            w1_copy(q - 1).wait()

            @pl.when(q + 1 < total)
            def _():
                w1_copy(q + 1).start()

            acc[...] += dot_nt(dab[prev], w1b[lax.rem(q - 1, RING)])
            dab[slot] = (gpb[slot] * dot_nt(recv[m], w2b[j])).astype(BF16)
            da_copy(m, j, slot).start()

            @pl.when(q + 2 < total)
            def _():
                gp_copy(q + 2).start()

            return 0

        lax.fori_loop(1, n_tile, tile, 0)

        q = m * n_tile + n_tile - 1
        w1_copy(q).wait()

        @pl.when(m < n_micro - 1)
        def _():
            w1_copy(q + 2).start()

        acc[...] += dot_nt(dab[lax.rem(q, 2)], w1b[lax.rem(q, RING)])
        h_copy(m).wait()

        @pl.when(m == 0)
        def _():
            pl.semaphore_wait(barrier, 1 + jnp.minimum(stage, 1) + jnp.minimum(last - stage, 1))

        peer_copy(m).start()

        @pl.when((stage > 0) & (m >= 2))
        def _():
            next_copy(m).wait_send()

        @pl.when((stage == 0) & (m >= 1))
        def _():
            x_copy(m).wait()

        oslot = lax.rem(m, 2)

        def norm_rows(i, dg):
            rows = pl.ds(pl.multiple_of(i * 16, 16), 16)
            r = hbuf[rows, :].astype(F32)
            inv = lax.rsqrt(jnp.mean(r * r, axis=-1, keepdims=True) + NORM_EPS)
            hat = r * inv
            dn = acc[rows, :]
            dg = dg + jnp.sum((dn * hat).reshape(2, 8, dn.shape[1]), axis=0)
            dgn = dn * g_ref[...]
            grad = recv[m, rows, :].astype(F32) + inv * (dgn - hat * jnp.mean(dgn * hat, axis=-1, keepdims=True))
            obuf[oslot, rows, :] = grad.astype(BF16)
            xbuf[rows, :] = grad
            return dg

        dg_ref[...] += lax.fori_loop(0, n_rows // 16, norm_rows, jnp.zeros(dg_ref.shape, F32))

        @pl.when(stage > 0)
        def _():
            next_copy(m).start()

        @pl.when(stage == 0)
        def _():
            x_copy(m).start()

        return 0

    lax.fori_loop(0, n_micro, micro, 0)

    for q in (total - 2, total - 1):
        da_copy(q // n_tile, q % n_tile, q % 2).wait()
    for m in range(n_micro):
        save_copy(m).wait()
        peer_copy(m).wait()

    @pl.when(stage > 0)
    def _():
        next_copy(n_micro - 2).wait_send()
        next_copy(n_micro - 1).wait_send()

    @pl.when(stage == 0)
    def _():
        x_copy(n_micro - 1).wait()


def backward(n_stage, top, hin, gain, w1, w2, gp):
    n_micro, n_tok, d = hin.shape
    f = w1.shape[1]
    n_tile = f // FB
    dma = pltpu.SemaphoreType.DMA
    act = jax.ShapeDtypeStruct(hin.shape, BF16)
    vmem = pl.BlockSpec(memory_space=pltpu.VMEM)
    return pl.pallas_call(
        functools.partial(bwd_kernel, n_stage, n_micro, n_tile),
        out_shape=(act, act,
                   jax.ShapeDtypeStruct((n_tile, n_micro, n_tok, FB), BF16),
                   jax.ShapeDtypeStruct(hin.shape, F32),
                   jax.ShapeDtypeStruct((8, d), F32)),
        in_specs=[ANY, ANY, vmem, ANY, ANY, ANY],
        out_specs=(ANY, ANY, ANY, ANY, vmem),
        scratch_shapes=[
            pltpu.VMEM((n_micro, n_tok, d), BF16),
            pltpu.VMEM((2, n_tok, d), BF16),
            pltpu.VMEM((n_tok, d), BF16),
            pltpu.VMEM((n_tok, d), F32),
            pltpu.VMEM((n_tok, d), F32),
            pltpu.VMEM((RING, d, FB), BF16),
            pltpu.VMEM((n_tile, FB, d), BF16),
            pltpu.VMEM((2, n_tok, FB), F32),
            pltpu.VMEM((2, n_tok, FB), BF16),
            dma((n_micro,)), dma((RING,)), dma((n_tile,)), dma((2,)), dma((2,)), dma, dma((n_micro,)), dma,
            dma((2,)), dma((n_micro,)), dma((n_micro,)), dma((n_micro,)),
        ],
        compiler_params=params(1),
        cost_estimate=cost(4 * n_micro * n_tok * d * f, 4 * d * f * (1 + n_micro)),
        name='backward',
    )(top, hin, gain, w1, w2, gp)


def logits_kernel(base_ref, h_ref, w_ref, lab_ref, z_ref, st_ref, m_s, s_s, t_s):
    i = pl.program_id(0)

    @pl.when(i == 0)
    def _():
        m_s[...] = jnp.full(m_s.shape, -jnp.inf, F32)
        s_s[...] = jnp.zeros(s_s.shape, F32)
        t_s[...] = jnp.zeros(t_s.shape, F32)

    z = dot_nt(h_ref[...], w_ref[...])
    z_ref[0] = z
    lane = lax.broadcasted_iota(jnp.int32, (1, 128), 1) + (base_ref[0] + i * VB)
    cols = [z[:, c:c + 128] for c in range(0, VB, 128)]
    m_old = m_s[...]
    m_new = m_old
    for part in cols:
        m_new = jnp.maximum(m_new, part)
    s_new = s_s[...] * jnp.exp(m_old - m_new)
    t_new = t_s[...]
    lab = lab_ref[...]
    for c, part in enumerate(cols):
        s_new = s_new + jnp.exp(part - m_new)
        t_new = t_new + jnp.where(lab == lane + c * 128, part, 0.0)
    m_s[...] = m_new
    s_s[...] = s_new
    t_s[...] = t_new

    @pl.when(i == pl.num_programs(0) - 1)
    def _():
        m_all = jnp.max(m_s[...], axis=1, keepdims=True)
        s_all = jnp.sum(s_s[...] * jnp.exp(m_s[...] - m_all), axis=1, keepdims=True)
        t_all = jnp.sum(t_s[...], axis=1, keepdims=True)
        col = lax.broadcasted_iota(jnp.int32, m_s.shape, 1)
        packed = jnp.where(col == 0, m_all, jnp.where(col == 1, s_all, t_all))
        st_ref[...] = packed.T[:8]


def logits(base, h, w, lab):
    n_tok, d = h.shape
    n_voc = w.shape[0]
    n_tile = n_voc // VB
    once = pl.Buffered(1)
    return pl.pallas_call(
        logits_kernel,
        out_shape=(jax.ShapeDtypeStruct((n_tile, n_tok, VB), F32), jax.ShapeDtypeStruct((8, n_tok), F32)),
        grid_spec=pltpu.PrefetchScalarGridSpec(
            num_scalar_prefetch=1,
            grid=(n_tile,),
            in_specs=[
                pl.BlockSpec((n_tok, d), lambda i, s: (0, 0), pipeline_mode=once),
                pl.BlockSpec((VB, d), lambda i, s: (i, 0)),
                pl.BlockSpec((n_tok, 128), lambda i, s: (0, 0), pipeline_mode=once),
            ],
            out_specs=(pl.BlockSpec((1, n_tok, VB), lambda i, s: (i, 0, 0)), pl.BlockSpec((8, n_tok), lambda i, s: (0, 0))),
            scratch_shapes=[pltpu.VMEM((n_tok, 128), F32)] * 3,
        ),
        compiler_params=params(),
        cost_estimate=cost(2 * n_tok * d * n_voc, 2 * d * n_voc + 4 * n_tok * n_voc),
        name='logits',
    )(base, h, w, lab)


def dz_of(z, lse, lab, lane, scale):
    parts = []
    for c in range(0, z.shape[1], 128):
        p = jnp.exp(z[:, c:c + 128] - lse)
        hot = jnp.where(lab == lane + c, 1.0, 0.0)
        parts.append(((p - hot) * scale).astype(BF16))
    return jnp.concatenate(parts, axis=1)


def dhid_kernel(scale, base_ref, z_ref, w_ref, lse_ref, lab_ref, dz_ref, dh_ref):
    i = pl.program_id(0)

    @pl.when(i == 0)
    def _():
        dh_ref[...] = jnp.zeros(dh_ref.shape, F32)

    lane = lax.broadcasted_iota(jnp.int32, (1, 128), 1) + (base_ref[0] + i * VB)
    dz = dz_of(z_ref[0], lse_ref[...], lab_ref[...], lane, scale)
    dz_ref[0] = dz
    dh_ref[...] += dot_nn(dz, w_ref[...])


def dhid(scale, half, n_half, base, z, w, lse, lab):
    n_tile, n_tok, _ = z.shape
    rows = n_tok // n_half
    n_voc, d = w.shape
    once = pl.Buffered(1)
    return pl.pallas_call(
        functools.partial(dhid_kernel, scale),
        out_shape=(jax.ShapeDtypeStruct((n_tile, rows, VB), BF16), jax.ShapeDtypeStruct((rows, d), F32)),
        grid_spec=pltpu.PrefetchScalarGridSpec(
            num_scalar_prefetch=1,
            grid=(n_tile,),
            in_specs=[
                pl.BlockSpec((1, rows, VB), lambda i, s: (i, half, 0)),
                pl.BlockSpec((VB, d), lambda i, s: (i, 0)),
                pl.BlockSpec((rows, 128), lambda i, s: (half, 0), pipeline_mode=once),
                pl.BlockSpec((rows, 128), lambda i, s: (half, 0), pipeline_mode=once),
            ],
            out_specs=(pl.BlockSpec((1, rows, VB), lambda i, s: (i, 0, 0)), pl.BlockSpec((rows, d), lambda i, s: (0, 0))),
        ),
        compiler_params=params(),
        cost_estimate=cost(2 * rows * d * n_voc, 2 * d * n_voc + 6 * rows * n_voc),
        name=f'dhid{half}',
    )(base, z, w, lse, lab)


def dwout_kernel(scale, s_ref, w_ref, dz0_ref, dz1_ref, ho_ref, hp_ref, lse_ref, lab_ref, *rest):
    out_ref = rest[-1]
    i = pl.program_id(0)

    @pl.when(i < s_ref[2])
    def _():
        rows = dz0_ref.shape[1]
        zp = dot_nt(hp_ref[...], w_ref[...])
        own = dot_tn(dz0_ref[0], ho_ref[:rows, :]) + dot_tn(dz1_ref[0], ho_ref[rows:, :])
        lane = lax.broadcasted_iota(jnp.int32, (1, 128), 1) + (s_ref[0] + (s_ref[1] + i) * VB)
        dzp = dz_of(zp, lse_ref[...], lab_ref[...], lane, scale)
        out_ref[...] = own + dot_tn(dzp, hp_ref[...])


def dwout(scale, n_step, scalars, w, dz0, dz1, ho, hp, lse, lab, out=None):
    n_voc, d = w.shape
    n_tok = ho.shape[0]
    rows = dz0.shape[1]
    once = pl.Buffered(1)

    def at(i, s):
        return jnp.minimum(s[1] + jnp.minimum(i, jnp.maximum(s[2] - 1, 0)), n_voc // VB - 1)

    more = [] if out is None else [out]
    return pl.pallas_call(
        functools.partial(dwout_kernel, scale),
        out_shape=jax.ShapeDtypeStruct((n_voc, d), F32),
        grid_spec=pltpu.PrefetchScalarGridSpec(
            num_scalar_prefetch=1,
            grid=(n_step,),
            in_specs=[
                pl.BlockSpec((VB, d), lambda i, s: (at(i, s), 0)),
                pl.BlockSpec((1, rows, VB), lambda i, s: (at(i, s), 0, 0)),
                pl.BlockSpec((1, rows, VB), lambda i, s: (at(i, s), 0, 0)),
                pl.BlockSpec((n_tok, d), lambda i, s: (0, 0), pipeline_mode=once),
                pl.BlockSpec((n_tok, d), lambda i, s: (0, 0), pipeline_mode=once),
                pl.BlockSpec((n_tok, 128), lambda i, s: (0, 0), pipeline_mode=once),
                pl.BlockSpec((n_tok, 128), lambda i, s: (0, 0), pipeline_mode=once),
            ] + [ANY] * len(more),
            out_specs=pl.BlockSpec((VB, d), lambda i, s: (at(i, s), 0)),
        ),
        input_output_aliases={} if out is None else {8: 0},
        compiler_params=params(),
        cost_estimate=cost(6 * n_tok * d * n_step * VB, (2 * d + 4 * d + 2 * n_tok) * n_step * VB),
        name='dwout_first' if out is None else 'dwout_rest',
    )(scalars, w, dz0, dz1, ho, hp, lse, lab, *more)


def wgrad_kernel(g_ref, ho_ref, hp_ref, dyo_ref, dyp_ref, w1_ref, w2_ref, u_ref, da_ref, dw1_ref, dw2_ref, nt_s, np_s):
    i = pl.program_id(0)
    n_tok = ho_ref.shape[0]

    @pl.when(i == 0)
    def _():
        def prep(src, base, keep):
            def rows_of(k, _):
                rows = pl.ds(pl.multiple_of(k * 128, 128), 128)
                r = src[rows, :].astype(F32)
                inv = lax.rsqrt(jnp.mean(r * r, axis=-1, keepdims=True) + NORM_EPS)
                n = (r * inv * g_ref[...]).astype(BF16)
                if keep:
                    np_s[rows, :] = n
                nt_s[:, pl.ds(pl.multiple_of(base + k * 128, 128), 128)] = n.T
                return 0

            lax.fori_loop(0, n_tok // 128, rows_of, 0)

        prep(ho_ref, 0, False)
        prep(hp_ref, n_tok, True)

    n_col = w1_ref.shape[1]
    a = dot_nn(np_s[...], w1_ref[...])
    dact = dot_nt(dyp_ref[...], w2_ref[...])
    u_own = u_ref[0].reshape(n_tok, n_col)
    da_own = da_ref[0].reshape(n_tok, n_col)
    dw2_own = dot_tn(u_own, dyo_ref[...])
    u, slope = gelu_and_slope(a)
    da = (slope * dact).astype(BF16)
    dw1_ref[...] = dot_nn(nt_s[:, :n_tok], da_own) + dot_nn(nt_s[:, n_tok:], da)
    dw2_ref[...] = dw2_own + dot_tn(u.astype(BF16), dyp_ref[...])


def wgrad(gain, ho, hp, dyo, dyp, w1, w2, u, da):
    n_tok, d = ho.shape
    f = w1.shape[1]
    per = FB // WB
    n_micro, n_row = u.shape[1:3]
    once = pl.Buffered(1)
    full = pl.BlockSpec((n_tok, d), lambda i: (0, 0), pipeline_mode=once)
    act = pl.BlockSpec((1, n_micro, n_row, WB), lambda i: (i // per, 0, 0, i % per))
    return pl.pallas_call(
        wgrad_kernel,
        out_shape=(jax.ShapeDtypeStruct((d, f), F32), jax.ShapeDtypeStruct((f, d), F32)),
        grid=(f // WB,),
        in_specs=[
            pl.BlockSpec((1, d), lambda i: (0, 0), pipeline_mode=once),
            full, full, full, full,
            pl.BlockSpec((d, WB), lambda i: (0, i)),
            pl.BlockSpec((WB, d), lambda i: (i, 0)),
            act, act,
        ],
        out_specs=(pl.BlockSpec((d, WB), lambda i: (0, i)), pl.BlockSpec((WB, d), lambda i: (i, 0))),
        scratch_shapes=[pltpu.VMEM((d, 2 * n_tok), BF16), pltpu.VMEM((n_tok, d), BF16)],
        compiler_params=params(),
        cost_estimate=cost(12 * n_tok * d * f, 12 * d * f + 4 * n_tok * f),
        name='wgrad',
    )(gain, ho, hp, dyo, dyp, w1, w2, u, da)


FIRST_TILES = (21, 18, 12, 9)


def solution(mesh):
    n_stage = mesh.shape['stage']
    n_dp = mesh.shape['dp']
    swap = [(0, 1), (1, 0)]

    def device_step(x_emb, labels, norm_gain, w_up, w_down, w_out):
        n_micro, n_tok, d = x_emb.shape
        own = n_micro * n_tok
        n_voc = w_out.shape[0]
        n_vtile = n_voc // VB
        stage = lax.axis_index('stage')
        dp = lax.axis_index('dp')
        scale = 1.0 / (own * n_dp)
        gain, w1, w2 = norm_gain[0], w_up[0, 0], w_down[0, 0]
        base = (stage * n_voc).reshape(1).astype(jnp.int32)

        def lanes(v):
            return jnp.broadcast_to(v.reshape(own, 1), (own, 128))

        lab = labels.reshape(own)
        lab_o, lab_p = lanes(lab), lanes(lax.ppermute(lab, 'dp', swap))

        hin, hinp, hfin, gp, u = forward(n_stage, x_emb, gain, w1, w2)
        ho = hfin.reshape(own, d)
        z, stats = logits(base, ho, w_out, lab_o)
        hp = lax.ppermute(ho, 'dp', swap)

        every = lax.all_gather(stats, ('dp', 'stage')).reshape(n_dp, n_stage, 8, own)
        top = jnp.max(every[:, :, 0], axis=1)
        lse = top + jnp.log(jnp.sum(every[:, :, 1] * jnp.exp(every[:, :, 0] - top[:, None]), axis=1))
        loss = jnp.sum(lse - jnp.sum(every[:, :, 2], axis=1)) * scale
        lse_o = lanes(lax.dynamic_index_in_dim(lse, dp, 0, keepdims=False))
        lse_p = lanes(lax.dynamic_index_in_dim(lse, 1 - dp, 0, keepdims=False))

        dzs, tops = [], []
        for half in range(2):
            dz, dh = dhid(scale, half, 2, base, z, w_out, lse_o, lab_o)
            dh = dh + lax.ppermute(dh, 'stage', [(0, 1), (2, 3)])
            dh = dh + lax.ppermute(dh, 'stage', [(1, 3)])
            dzs.append(dz)
            tops.append(dh.astype(BF16))
        dtop = jnp.concatenate(tops, axis=0).reshape(n_micro, n_tok, d)

        first = jnp.asarray(FIRST_TILES, jnp.int32)[stage].reshape(1)
        s_first = jnp.concatenate([base, jnp.zeros((1,), jnp.int32), first])
        s_rest = jnp.concatenate([base, first, n_vtile - first])
        head = (w_out, dzs[0], dzs[1], ho, hp, lse_p, lab_p)
        gw = dwout(scale, max(FIRST_TILES), s_first, *head)

        dtop, gw = lax.optimization_barrier((dtop, gw))
        dyin, dyp, da, gx, dg = backward(n_stage, dtop, hin, gain, w1, w2, gp)
        gw, dyin = lax.optimization_barrier((gw, dyin))
        gw = dwout(scale, n_vtile - min(FIRST_TILES), s_rest, *head, out=gw)

        gw, gx, dg, dyin = lax.optimization_barrier((gw, gx, dg, dyin))
        dw1, dw2 = wgrad(gain, hin.reshape(own, d), hinp.reshape(own, d), dyin.reshape(own, d), dyp.reshape(own, d), w1, w2, u, da)

        dg = jnp.sum(dg, axis=0)
        dg = dg + lax.ppermute(dg, 'dp', swap)
        width = d // n_stage
        grad_x = jnp.where(stage == 0, gx[:, :, :width], 0.0)
        for k in range(1, n_stage):
            grad_x = grad_x + lax.ppermute(gx[:, :, k * width:(k + 1) * width], 'stage', [(0, k)])
        return loss.reshape(1), grad_x, dg.reshape(1, 1, d), dw1[None, None], dw2[None, None], gw

    tok_spec = ('pod', 'dp')
    stage_spec = ('pod', 'stage')
    in_specs = (P(None, tok_spec, None), P(None, tok_spec), P(stage_spec, None, None), P(stage_spec, None, None, None), P(stage_spec, None, None, None), P(stage_spec, None))
    out_specs = (P('pod'), P(None, tok_spec, 'stage'), P(stage_spec, None, None), P(stage_spec, None, None, None), P(stage_spec, None, None, None), P(stage_spec, None))
    return jax.shard_map(device_step, mesh=mesh, in_specs=in_specs, out_specs=out_specs, check_vma=False)
```

time: 7620 us -> 1090 us (0.14)
  waiting for transfers between devices: 5260 us -> 63.6 us
  matrix products: 1660 us -> 0 us
  Pallas kernels: 0 us -> 922 us
  local copies, waits for them, and re-layouts: 230 us -> 11 us
  blocking collectives: 200 us -> 24 us
  other arithmetic: 133 us -> 34.4 us
    psum x4 -> x0, waiting for transfers between devices: 5180 us -> none  [the longest x3 5090 us: device_step(): lax.psum((bwd_state[1], bwd_state[2], bwd_state[3], acc_out), 'dp')]
    dot_general x54 -> x0, matrix products: 1660 us -> none  [the longest x7 325 us: block_backward(): jnp.einsum('tf,td->fd', act_bf16, grad_out, preferred_element_type=jnp.fl...]
    pallas_call x0 -> x8, Pallas kernels: none -> 922 us  [the longest x1 242 us: wgrad(): pl.pallas_call(wgrad_kernel, out_shape=(jax.ShapeDtypeStruct((d, f), F32)...]
    psum x6 -> x0, blocking collectives: 176 us -> none  [the longest x1 146 us: device_step(): d_top = lax.psum(d_hid, 'stage').astype(jnp.bfloat16)]
    unnamed x9 -> x5, local copies, waits for them, and re-layouts: 152 us -> 0.7 us
  transfers between devices with their start and end apart: 19 -> 10, of which waited for: 12 -> 1; matrix products, arithmetic and copies ran while one was open for 9% -> 3% of each run, Pallas kernels for 0% -> 41%
where the time goes in v1:
time: 1090 us; the launch traced here: 1080 us
  Pallas kernels  922 us (85%)
  waiting for transfers between devices  63.6 us (6%)
  other arithmetic  34.4 us (3%)
  starting transfers between devices  26.6 us (2%)
  blocking collectives  24 us (2%)
  local copies, waits for them, and re-layouts  11 us (1%)
    pallas_call x1, Pallas kernels, wgrad(): pl.pallas_call(wgrad_kernel, out_shape=(jax.ShapeDtypeStruct((d, f), F32)...  242 us
    pallas_call x1, Pallas kernels, forward(): pl.pallas_call(functools.partial(fwd_kernel, n_stage, n_micro, n_tile), o...  211 us
    pallas_call x2, Pallas kernels, dwout(): pl.pallas_call(functools.partial(dwout_kernel, scale), out_shape=jax.Shap...  186 us
    pallas_call x1, Pallas kernels, backward(): pl.pallas_call(functools.partial(bwd_kernel, n_stage, n_micro, n_tile), o...  121 us
    pallas_call x2, Pallas kernels, dhid(): pl.pallas_call(functools.partial(dhid_kernel, scale), out_shape=(jax.Shap...  89.5 us
    pallas_call x1, Pallas kernels, logits(): pl.pallas_call(logits_kernel, out_shape=(jax.ShapeDtypeStruct((n_tile, n_...  72 us
    ppermute x1, waiting for transfers between devices, device_step(): lab_o, lab_p = (lanes(lab), lanes(lax.ppermute(lab, 'dp', swap)))  63.5 us
    all_gather x1, blocking collectives, device_step(): lax.all_gather(stats, ('dp', 'stage')).reshape(n_dp, n_stage, 8, own)  24 us
  transfers between devices with their start and end apart: 10, of which 1 were waited for; matrix products, arithmetic and copies ran while one was open for 3% of the time, Pallas kernels for 41%

profile of v1, /device:TPU:0, one launch (start us, length us, event | category | flops | bytes accessed | tf_op | source)
XLA Modules:
  0.0 1084.7 jit_solution(2747126396584784279)
XLA Ops:
  0.6 0.7 copy.18
  1.3 211.2 %forward.1 = (bf16[4,256,2048]{2,1,0:T(8,128)(2,1)}, bf16[4,256,2048]{2,1,0:T(8,128)(2,1)}, bf16[4,256,2048]{2,1,0:T(8,128)(2,1)}, f32[4,8,256,1024]{3,2,1,0:T(8,128)}, bf16[8,4,256,1024]{3,2,1,0:T(8,128)(2,1)}) custom-call(bf16[4,256,2048]{2,1,0:T(8,128)(2,1)} %x_ref.1, f32[1,2048]{1,0:T(1,128)} %bitcast.49, bf16[2048,8192]{1,0:T(8,128)(2,1)} %bitcast.39, ...), custom_call_target="tpu_custom_call" | custom-call | flops 68719476736 | bytes 335544320 | tf_op jit(solution)/shard_map/forward/pallas_call | solution.py:234
  212.5 1.0 broadcast_in_dim.38.lab_ref
  213.5 72.0 %logits.1 = (f32[24,1024,512]{2,1,0:T(8,128)}, f32[8,1024]{1,0:T(8,128)}) custom-call(s32[1]{0:T(128)} %bitcast.base_ref, bf16[1024,2048]{1,0:T(8,128)(2,1)} %bitcast.45, bf16[12288,2048]{1,0:T(8,128)(2,1)} %w_ref.9, s32[1024,128]{1,0:T(8,128)} %broadcast_in_dim.38.lab_ref), custom_call_target="tpu_custom_call" | custom-call | flops 51539607552 | bytes 100663296 | tf_op jit(solution)/shard_map/logits/pallas_call | solution.py:531
  285.5 24.0 %all-gather = f32[64,1024]{1,0:T(8,128)S(1)} all-gather(f32[8,1024]{1,0:T(8,128)} %get-tuple-element.33), channel_id=2, replica_groups=mesh['pod'=1,'dp'=2,'stage'=4] {'dp','stage'}, dimensions={0}, use_global_device_ids=true | all-gather | bytes 294912 | tf_op jit(solution)/shard_map/all_gather | solution.py:737
  309.4 0.1 slice_reduce_fusion
  309.6 0.6 subtract_reduce_fusion
  310.2 1.0 broadcast_in_dim.40.lse_ref
  311.2 44.8 %dhid1.1 = (bf16[24,512,512]{2,1,0:T(8,128)(2,1)}, f32[512,2048]{1,0:T(8,128)}) custom-call(s32[1]{0:T(128)} %bitcast.base_ref, f32[24,1024,512]{2,1,0:T(8,128)} %get-tuple-element.34.z_ref, bf16[12288,2048]{1,0:T(8,128)(2,1)} %w_ref.9, f32[1024,128]{1,0:T(8,128)} %broadcast_in_dim.40.lse_ref, s32[1024,128]{1,0:T(8,128)} %broadcast_in_dim.38.lab_ref), custom_call_target="tpu_custom_call" | custom-call | flops 25769803776 | bytes 88080384 | tf_op jit(solution)/shard_map/dhid1/pallas_call | solution.py:578
  356.0 0.0 copy-start.1
  356.0 3.3 collective-permute-start.4
  359.3 44.7 %dhid0.1 = (bf16[24,512,512]{2,1,0:T(8,128)(2,1)}, f32[512,2048]{1,0:T(8,128)}) custom-call(s32[1]{0:T(128)} %bitcast.base_ref, f32[24,1024,512]{2,1,0:T(8,128)} %get-tuple-element.34.z_ref, bf16[12288,2048]{1,0:T(8,128)(2,1)} %w_ref.9, f32[1024,128]{1,0:T(8,128)} %broadcast_in_dim.40.lse_ref, s32[1024,128]{1,0:T(8,128)} %broadcast_in_dim.38.lab_ref), custom_call_target="tpu_custom_call" | custom-call | flops 25769803776 | bytes 88080384 | tf_op jit(solution)/shard_map/dhid0/pallas_call | solution.py:578
  404.0 3.5 collective-permute-start.2
  407.5 0.1 collective-permute-start
  407.6 2.0 collective-permute-start.1
  409.6 0.0 copy-done.1
  409.6 0.6 dynamic_slice.10
  410.8 1.2 pad_add_fusion.s_ref
  412.0 1.3 pad_add_fusion.1.s_ref
  414.0 0.0 copy-start
  414.0 0.0 collective-permute-done.4
  414.0 6.7 add.44
  420.7 2.6 collective-permute-start.5
  423.3 0.0 collective-permute-done.2
  423.3 0.0 copy-done
  423.3 4.9 add.42
  428.2 2.7 collective-permute-start.3
  431.0 63.5 %collective-permute-done.1 = s32[1024]{0:T(1024)S(1)} collective-permute-done((s32[1024]{0:T(1024)S(1)}, s32[1024]{0:T(1024)S(1)}, u32[]{:S(2)}, u32[]{:S(2)}) %collective-permute-start.1) | collective-permute-done | bytes 4128 | tf_op jit(solution)/shard_map/ppermute | solution.py:730
  494.5 0.0 collective-permute-done.hp_ref
  494.5 1.0 broadcast_in_dim.43.lab_ref
  495.5 1.0 broadcast_in_dim.42.lse_ref
  496.5 156.0 %dwout_first.1.rest_0_ = f32[12288,2048]{1,0:T(8,128)} custom-call(s32[3]{0:T(128)} %pad_add_fusion.1.s_ref, bf16[12288,2048]{1,0:T(8,128)(2,1)} %w_ref.9, bf16[24,512,512]{2,1,0:T(8,128)(2,1)} %get-tuple-element.35.dz0_ref, bf16[24,512,512]{2,1,0:T(8,128)(2,1)} %get-tuple-element.36.dz1_ref, bf16[1024,2048]{1,0:T(8,128)(2,1)} %bitcast.47, ...), custom_call_target="tpu_custom_call" | custom-call | flops 135291469824 | bytes 154140672 | tf_op jit(solution)/shard_map/dwout_first/pallas_call | solution.py:622
  652.5 0.0 collective-permute-done.5
  652.5 4.1 add_convert_fusion
  656.6 0.0 collective-permute-done.3
  656.6 4.1 add_convert_fusion.1
  660.7 2.6 pad_maximum_fusion
  663.3 121.3 %backward.1 = (bf16[4,256,2048]{2,1,0:T(8,128)(2,1)}, bf16[4,256,2048]{2,1,0:T(8,128)(2,1)}, bf16[8,4,256,1024]{3,2,1,0:T(8,128)(2,1)}, f32[4,256,2048]{2,1,0:T(8,128)}, f32[8,2048]{1,0:T(8,128)}) custom-call(bf16[4,256,2048]{2,1,0:T(8,128)(2,1)} %bitcast.31, bf16[4,256,2048]{2,1,0:T(8,128)(2,1)} %get-tuple-element.41.hin_ref, f32[1,2048]{1,0:T(1,128)} %bitcast.50, ...), custom_call_target="tpu_custom_call" | custom-call | flops 68719476736 | bytes 335544320 | tf_op jit(solution)/shard_map/backward/pallas_call | solution.py:462
  784.6 29.6 %dwout_rest.1 = f32[12288,2048]{1,0:T(8,128)} custom-call(s32[3]{0:T(128)} %pad_add_fusion.s_ref, bf16[12288,2048]{1,0:T(8,128)(2,1)} %w_ref.9, bf16[24,512,512]{2,1,0:T(8,128)(2,1)} %get-tuple-element.35.dz0_ref, bf16[24,512,512]{2,1,0:T(8,128)(2,1)} %get-tuple-element.36.dz1_ref, bf16[1024,2048]{1,0:T(8,128)(2,1)} %bitcast.48, ...), custom_call_target="tpu_custom_call", output_to_operand_aliasing={{}: (8, {})} | custom-call | flops 96636764160 | bytes 110100480 | tf_op jit(solution)/shard_map/dwout_rest/pallas_call | solution.py:622
  814.2 1.5 reduce_sum.39
  815.7 0.0 collective-permute-start.9
  815.7 5.8 fusion.4
  821.4 6.9 collective-permute-start.6
  828.4 2.6 collective-permute-start.8
  831.0 2.8 collective-permute-start.7
  833.8 242.1 %wgrad.1 = (f32[2048,8192]{1,0:T(8,128)}, f32[8192,2048]{1,0:T(8,128)}) custom-call(f32[1,2048]{1,0:T(1,128)} %bitcast.51, bf16[1024,2048]{1,0:T(8,128)(2,1)} %bitcast.52, bf16[1024,2048]{1,0:T(8,128)(2,1)} %bitcast.53, bf16[1024,2048]{1,0:T(8,128)(2,1)} %bitcast.54, bf16[1024,2048]{1,0:T(8,128)(2,1)} %bitcast.55, bf16[2048,8192]{1,0:T(8,128)(2,1)} %bitcast.41, ...), custom_call_target="tpu_custom_call" | custom-call | flops 206158430208 | bytes 234881024 | tf_op jit(solution)/shard_map/wgrad/pallas_call | solution.py:688
  1075.9 0.0 collective-permute-done.9
  1075.9 1.3 add.49
  1077.2 0.0 collective-permute-done.6
  1077.2 0.0 collective-permute-done.8
  1077.2 0.0 collective-permute-done.7
  1077.2 5.9 add_add_fusion
  (2 shorter events, 0.1 us)
Async XLA Ops:
  356.0 53.5 %copy-start.1 = (s32[4]{0:T(128)S(1)}, s32[4]{0:T(128)}, u32[]{:S(2)}) copy-start(s32[4]{0:T(128)} %constant.38.clone) | copy-start | bytes 52
  356.0 57.9 %collective-permute-start.4 = (f32[512,2048]{1,0:T(8,128)}, f32[512,2048]{1,0:T(8,128)}, u32[]{:S(2)}, u32[]{:S(2)}) collective-permute-start(f32[512,2048]{1,0:T(8,128)} %get-tuple-element.38), channel_id=1, source_target_pairs={{0,1},{2,3},{4,5},{6,7}} | collective-permute-start | bytes 12582920 | tf_op jit(solution)/shard_map/ppermute | solution.py:747
  404.0 19.3 %collective-permute-start.2 = (f32[512,2048]{1,0:T(8,128)}, f32[512,2048]{1,0:T(8,128)}, u32[]{:S(2)}, u32[]{:S(2)}) collective-permute-start(f32[512,2048]{1,0:T(8,128)} %get-tuple-element.37), channel_id=1, source_target_pairs={{0,1},{2,3},{4,5},{6,7}} | collective-permute-start | bytes 12582920 | tf_op jit(solution)/shard_map/ppermute | solution.py:747
  407.5 87.0 %collective-permute-start = (bf16[1024,2048]{1,0:T(8,128)(2,1)}, bf16[1024,2048]{1,0:T(8,128)(2,1)}, u32[]{:S(2)}, u32[]{:S(2)}) collective-permute-start(bf16[1024,2048]{1,0:T(8,128)(2,1)} %bitcast.46), channel_id=1, source_target_pairs={{0,4},{4,0},{1,5},{5,1},{2,6},{6,2},{3,7},{7,3}} | collective-permute-start | bytes 12582920 | tf_op jit(solution)/shard_map/ppermute | solution.py:735
  407.6 86.9 %collective-permute-start.1 = (s32[1024]{0:T(1024)S(1)}, s32[1024]{0:T(1024)S(1)}, u32[]{:S(2)}, u32[]{:S(2)}) collective-permute-start(s32[1024]{0:T(1024)S(1)} %bitcast.36), channel_id=1, source_target_pairs={{0,4},{4,0},{1,5},{5,1},{2,6},{6,2},{3,7},{7,3}} | collective-permute-start | bytes 12296 | tf_op jit(solution)/shard_map/ppermute | solution.py:730
  414.0 9.4 copy-start
  420.7 231.8 %collective-permute-start.5 = (f32[512,2048]{1,0:T(8,128)}, f32[512,2048]{1,0:T(8,128)}, u32[]{:S(2)}, u32[]{:S(2)}) collective-permute-start(f32[512,2048]{1,0:T(8,128)} %add.44), channel_id=1, source_target_pairs={{1,3},{5,7}} | collective-permute-start | bytes 12582920 | tf_op jit(solution)/shard_map/ppermute | solution.py:748
  428.2 228.4 %collective-permute-start.3 = (f32[512,2048]{1,0:T(8,128)}, f32[512,2048]{1,0:T(8,128)}, u32[]{:S(2)}, u32[]{:S(2)}) collective-permute-start(f32[512,2048]{1,0:T(8,128)} %add.42), channel_id=1, source_target_pairs={{1,3},{5,7}} | collective-permute-start | bytes 12582920 | tf_op jit(solution)/shard_map/ppermute | solution.py:748
  815.7 260.2 %collective-permute-start.9 = (f32[2048]{0:T(1024)}, f32[2048]{0:T(1024)}, u32[]{:S(2)}, u32[]{:S(2)}) collective-permute-start(f32[2048]{0:T(1024)} %reduce_sum.39), channel_id=1, source_target_pairs={{0,4},{4,0},{1,5},{5,1},{2,6},{6,2},{3,7},{7,3}} | collective-permute-start | bytes 24584 | tf_op jit(solution)/shard_map/ppermute | solution.py:768
  821.4 255.8 %collective-permute-start.6 = (f32[4,256,512]{2,1,0:T(8,128)}, f32[4,256,512]{2,1,0:T(8,128)}, u32[]{:S(2)}, u32[]{:S(2)}) collective-permute-start(f32[4,256,512]{2,1,0:T(8,128)} %get-tuple-element.62), channel_id=1, source_target_pairs={{0,1},{4,5}} | collective-permute-start | bytes 6291464 | tf_op jit(solution)/shard_map/ppermute | solution.py:772
  828.4 248.8 %collective-permute-start.8 = (f32[4,256,512]{2,1,0:T(8,128)}, f32[4,256,512]{2,1,0:T(8,128)}, u32[]{:S(2)}, u32[]{:S(2)}) collective-permute-start(f32[4,256,512]{2,1,0:T(8,128)} %get-tuple-element.63), channel_id=1, source_target_pairs={{0,3},{4,7}} | collective-permute-start | bytes 6291464 | tf_op jit(solution)/shard_map/ppermute | solution.py:772
  831.0 246.2 %collective-permute-start.7 = (f32[4,256,512]{2,1,0:T(8,128)}, f32[4,256,512]{2,1,0:T(8,128)}, u32[]{:S(2)}, u32[]{:S(2)}) collective-permute-start(f32[4,256,512]{2,1,0:T(8,128)} %get-tuple-element.64), channel_id=1, source_target_pairs={{0,2},{4,6}} | collective-permute-start | bytes 6291464 | tf_op jit(solution)/shard_map/ppermute | solution.py:772

commit v2 on v1

v2 whole, which is shorter than its diff:
```python
import functools

import jax
import jax.numpy as jnp
from jax import lax
from jax.experimental import pallas as pl
from jax.experimental.pallas import tpu as pltpu
from jax.sharding import PartitionSpec as P


NORM_EPS = 1e-6
FB = 512
WB = 256
VB = 512
RING = 6
LANES = 128
ROWS = 32
GELU_C = 0.7978845608028654
GELU_K = 0.044715
VMEM_LIMIT = 67_000_000
MESH = pl.DeviceIdType.MESH
F32 = jnp.float32
BF16 = jnp.bfloat16
ANY = pl.BlockSpec(memory_space=pl.ANY)


def dot_nn(a, b):
    return jnp.dot(a[...], b[...], preferred_element_type=F32)


def dot_nt(a, b):
    return lax.dot_general(a[...], b[...], (((1,), (1,)), ((), ())), preferred_element_type=F32)


def dot_tn(a, b):
    return lax.dot_general(a[...], b[...], (((0,), (0,)), ((), ())), preferred_element_type=F32)


def gelu_and_slope(a):
    sq = a * a
    t = jnp.tanh(a * (GELU_C + (GELU_C * GELU_K) * sq))
    cdf = 0.5 + 0.5 * t
    slope = cdf + a * ((0.5 - 0.5 * (t * t)) * (GELU_C + (3.0 * GELU_C * GELU_K) * sq))
    return a * cdf, slope


def home(*_):
    return 0, 0


def params(collective_id=None, **more):
    return pltpu.CompilerParams(
        vmem_limit_bytes=VMEM_LIMIT,
        collective_id=collective_id,
        has_side_effects=collective_id is not None,
        **more,
    )


def cost(flops, bytes_accessed):
    return pl.CostEstimate(flops=int(flops), bytes_accessed=int(bytes_accessed), transcendentals=0)


def fwd_kernel(n_stage, n_micro, n_tile, x_ref, g_ref, w1_ref, w2_ref, hin_ref, hinp_ref, hfin_ref, gp_ref, u_ref,
               recv, obuf, norm, acc, w1b, w2b, gpb, uob, ua, ub,
               x_sem, w1_sem, w2_sem, gp_sem, u_sem, hs_sem, fin_sem, send_sem, recv_sem, psend_sem, precv_sem, bsend_sem, frecv_sem):
    stage = lax.axis_index('stage')
    dp = lax.axis_index('dp')
    last = n_stage - 1
    n_rows = recv.shape[1]
    total = n_micro * n_tile
    n_pair = n_tile // 2

    barrier = pltpu.get_barrier_semaphore()
    for step in range(1, n_stage):
        pl.semaphore_signal(barrier, inc=1, device_id={'stage': lax.rem(stage + step, n_stage)}, device_id_type=MESH)
    pl.semaphore_signal(barrier, inc=1, device_id={'dp': 1 - dp}, device_id_type=MESH)

    def x_copy(m):
        return pltpu.make_async_copy(x_ref.at[m], recv.at[m], x_sem.at[m])

    def w1_copy(j):
        return pltpu.make_async_copy(w1_ref.at[:, pl.ds(pl.multiple_of(j * FB, FB), FB)], w1b.at[j], w1_sem.at[j])

    def w2_copy(q):
        slot = lax.rem(q, RING)
        j = lax.rem(q, n_tile)
        return pltpu.make_async_copy(w2_ref.at[pl.ds(pl.multiple_of(j * FB, FB), FB), :], w2b.at[slot], w2_sem.at[slot])

    def out_copies(m, j, slot, side):
        return (pltpu.make_async_copy(gpb.at[slot, side], gp_ref.at[m, j], gp_sem.at[slot, side]),
                pltpu.make_async_copy(uob.at[slot, side], u_ref.at[j, m], u_sem.at[slot, side]))

    def save_copy(m):
        return pltpu.make_async_copy(recv.at[m], hin_ref.at[m], hs_sem.at[m])

    def peer_copy(m):
        return pltpu.make_async_remote_copy(recv.at[m], hinp_ref.at[m], psend_sem.at[m], precv_sem.at[m],
                                            device_id={'dp': 1 - dp}, device_id_type=MESH)

    def next_copy(m):
        return pltpu.make_async_remote_copy(obuf.at[m], recv.at[m], send_sem.at[m], recv_sem.at[m],
                                            device_id={'stage': lax.rem(stage + 1, n_stage)}, device_id_type=MESH)

    def fin_copy(m):
        return pltpu.make_async_copy(obuf.at[m], hfin_ref.at[m], fin_sem.at[m])

    def bcast_copy(m, k):
        return pltpu.make_async_remote_copy(obuf.at[m], hfin_ref.at[m], bsend_sem.at[m, k], frecv_sem.at[m],
                                            device_id={'stage': k}, device_id_type=MESH)

    def relay_copy(m):
        return pltpu.make_async_remote_copy(hfin_ref.at[m], hfin_ref.at[m], bsend_sem.at[m, 0], frecv_sem.at[m],
                                            device_id={'stage': 0}, device_id_type=MESH)

    w1_copy(0).start()
    w1_copy(1).start()
    w2_copy(0).start()

    @pl.when(stage == 0)
    def _():
        for m in range(n_micro):
            x_copy(m).start()

    for j in range(2, n_tile):
        w1_copy(j).start()
        if j < RING - 1:
            w2_copy(j - 1).start()
    pl.semaphore_wait(barrier, n_stage)

    def ahead(m, j):
        @pl.when(m == 0)
        def _():
            w1_copy(j).wait()

    def refill(q):
        w2_copy(q).wait()

        @pl.when(q + RING - 2 < total)
        def _():
            w2_copy(q + RING - 2).start()

    def hidden(j, slot, side, keep):
        u, slope = gelu_and_slope(dot_nn(norm, w1b[j]))
        gpb[slot, side] = slope
        u = u.astype(BF16)
        uob[slot, side] = u
        keep[...] = u

    def free(slot, side):
        for copy in out_copies(0, 0, slot, side):
            copy.wait()

    def put(m, j, slot, side):
        for copy in out_copies(m, j, slot, side):
            copy.start()

    @pl.loop(0, n_micro)
    def _(m):
        @pl.when(stage == 0)
        def _():
            x_copy(m).wait()

        @pl.when(stage > 0)
        def _():
            next_copy(m).wait_recv()

        save_copy(m).start()
        peer_copy(m).start()

        @pl.loop(0, n_rows, step=ROWS)
        def _(i):
            rows = pl.ds(pl.multiple_of(i, ROWS), ROWS)
            r = recv[m, rows, :].astype(F32)
            inv = lax.rsqrt(jnp.mean(r * r, axis=-1, keepdims=True) + NORM_EPS)
            norm[rows, :] = (r * inv * g_ref[...]).astype(BF16)
            acc[rows, :] = r

        k0 = m * n_pair
        ahead(m, 0)

        @pl.when(k0 >= 2)
        def _():
            free(lax.rem(k0, 2), 0)

        hidden(0, lax.rem(k0, 2), 0, ua)
        put(m, 0, lax.rem(k0, 2), 0)

        @pl.loop(1, n_pair)
        def _(k):
            slot = lax.rem(k0 + k, 2)
            j = 2 * k
            q = m * n_tile + j
            ahead(m, j - 1)
            ahead(m, j)
            refill(q - 2)
            refill(q - 1)

            @pl.when(k0 + k >= 2)
            def _():
                free(slot, 0)

            @pl.when(k0 + k >= 3)
            def _():
                free(slot, 1)

            hidden(j - 1, slot, 1, ub)
            acc[...] += dot_nn(ua, w2b[lax.rem(q - 2, RING)])
            hidden(j, slot, 0, ua)
            acc[...] += dot_nn(ub, w2b[lax.rem(q - 1, RING)])
            put(m, j - 1, slot, 1)
            put(m, j, slot, 0)

        slot = lax.rem(k0 + n_pair, 2)
        q = m * n_tile + n_tile - 1
        ahead(m, n_tile - 1)
        refill(q - 1)
        refill(q)

        @pl.when(k0 + n_pair >= 3)
        def _():
            free(slot, 1)

        hidden(n_tile - 1, slot, 1, ub)
        acc[...] += dot_nn(ua, w2b[lax.rem(q - 1, RING)])
        obuf[m] = (acc[...] + dot_nn(ub, w2b[lax.rem(q, RING)])).astype(BF16)

        @pl.when(stage < last)
        def _():
            next_copy(m).start()

        @pl.when(stage == last)
        def _():
            for k in range(last - 1, 0, -1):
                bcast_copy(m, k).start()
            fin_copy(m).start()

        put(m, n_tile - 1, slot, 1)

    for side in range(2):
        for slot in range(2):
            free(slot, side)

    @pl.when(stage < last)
    def _():
        for m in range(n_micro):
            bcast_copy(m, 1).wait_recv()

            @pl.when(stage == 1)
            def _():
                relay_copy(m).start()

    for m in range(n_micro):
        save_copy(m).wait()
        peer_copy(m).wait()

        @pl.when(stage < last)
        def _():
            next_copy(m).wait_send()

        @pl.when(stage == 1)
        def _():
            relay_copy(m).wait_send()

        @pl.when(stage == last)
        def _():
            fin_copy(m).wait()
            for k in range(1, last):
                bcast_copy(m, k).wait_send()


def forward(n_stage, x, gain, w1, w2):
    n_micro, n_tok, d = x.shape
    f = w1.shape[1]
    n_tile = f // FB
    dma = pltpu.SemaphoreType.DMA
    act = jax.ShapeDtypeStruct(x.shape, BF16)
    return pl.pallas_call(
        functools.partial(fwd_kernel, n_stage, n_micro, n_tile),
        out_shape=(act, act, act,
                   jax.ShapeDtypeStruct((n_micro, n_tile, n_tok, FB), F32),
                   jax.ShapeDtypeStruct((n_tile, n_micro, n_tok, FB), BF16)),
        in_specs=[ANY, pl.BlockSpec(memory_space=pltpu.VMEM), ANY, ANY],
        out_specs=(ANY,) * 5,
        scratch_shapes=[
            pltpu.VMEM((n_micro, n_tok, d), BF16),
            pltpu.VMEM((n_micro, n_tok, d), BF16),
            pltpu.VMEM((n_tok, d), BF16),
            pltpu.VMEM((n_tok, d), F32),
            pltpu.VMEM((n_tile, d, FB), BF16),
            pltpu.VMEM((RING, FB, d), BF16),
            pltpu.VMEM((2, 2, n_tok, FB), F32),
            pltpu.VMEM((2, 2, n_tok, FB), BF16),
            pltpu.VMEM((n_tok, FB), BF16),
            pltpu.VMEM((n_tok, FB), BF16),
            dma((n_micro,)), dma((n_tile,)), dma((RING,)), dma((2, 2)), dma((2, 2)), dma((n_micro,)), dma((n_micro,)),
            dma((n_micro,)), dma((n_micro,)), dma((n_micro,)), dma((n_micro,)), dma((n_micro, n_stage - 1)), dma((n_micro,)),
        ],
        compiler_params=params(0),
        cost_estimate=cost(4 * n_micro * n_tok * d * f, 4 * d * f * (1 + n_micro)),
        name='forward',
    )(x, gain, w1, w2)


def bwd_kernel(n_stage, n_micro, n_tile, top0_ref, top1_ref, hin_ref, g_ref, w1_ref, w2_ref, gp_ref,
               dyin_ref, dyp_ref, da_ref, gx_ref, dg_ref,
               recv, obuf, hbuf, acc, xbuf, w1b, w2b, gpb, dob, da_a, da_b,
               t_sem, w1_sem, w2_sem, gp_sem, da_sem, h_sem, hs_sem, x_sem, send_sem, recv_sem, psend_sem, precv_sem):
    stage = lax.axis_index('stage')
    dp = lax.axis_index('dp')
    last = n_stage - 1
    n_rows, d = recv.shape[1:]
    total = n_micro * n_tile
    n_pair = n_tile // 2

    barrier = pltpu.get_barrier_semaphore()
    pl.semaphore_signal(barrier, inc=1, device_id={'dp': 1 - dp}, device_id_type=MESH)

    @pl.when(stage > 0)
    def _():
        pl.semaphore_signal(barrier, inc=1, device_id={'stage': stage - 1}, device_id_type=MESH)

    @pl.when(stage < last)
    def _():
        pl.semaphore_signal(barrier, inc=1, device_id={'stage': stage + 1}, device_id_type=MESH)

    def top_copy(m):
        half = n_micro // 2
        top_ref = top0_ref if m < half else top1_ref
        return pltpu.make_async_copy(top_ref.at[m % half], recv.at[m], t_sem.at[m])

    def w2_copy(j):
        return pltpu.make_async_copy(w2_ref.at[pl.ds(pl.multiple_of(j * FB, FB), FB), :], w2b.at[j], w2_sem.at[j])

    def w1_copy(q):
        slot = lax.rem(q, RING)
        j = lax.rem(q, n_tile)
        return pltpu.make_async_copy(w1_ref.at[:, pl.ds(pl.multiple_of(j * FB, FB), FB)], w1b.at[slot], w1_sem.at[slot])

    def gp_copy(q):
        slot = lax.rem(q, 4)
        return pltpu.make_async_copy(gp_ref.at[lax.div(q, n_tile), lax.rem(q, n_tile)], gpb.at[slot], gp_sem.at[slot])

    def da_copy(m, j, slot, side):
        return pltpu.make_async_copy(dob.at[slot, side], da_ref.at[j, m], da_sem.at[slot, side])

    def h_copy(m):
        return pltpu.make_async_copy(hin_ref.at[m], hbuf, h_sem)

    def save_copy(m):
        return pltpu.make_async_copy(recv.at[m], dyin_ref.at[m], hs_sem.at[m])

    def peer_copy(m):
        return pltpu.make_async_remote_copy(recv.at[m], dyp_ref.at[m], psend_sem.at[m], precv_sem.at[m],
                                            device_id={'dp': 1 - dp}, device_id_type=MESH)

    def next_copy(m):
        slot = lax.rem(m, 2)
        return pltpu.make_async_remote_copy(obuf.at[slot], recv.at[m], send_sem.at[slot], recv_sem.at[m],
                                            device_id={'stage': lax.rem(stage + last, n_stage)}, device_id_type=MESH)

    def x_copies(m):
        width = d // n_stage
        return [pltpu.make_async_copy(xbuf.at[:, pl.ds(k * width, width)], gx_ref.at[k, m], x_sem.at[k]) for k in range(n_stage)]

    @pl.when(stage == last)
    def _():
        for m in range(n_micro):
            top_copy(m).start()

    w2_copy(0).start()
    for q in range(4):
        gp_copy(q).start()
    w2_copy(1).start()
    w2_copy(2).start()
    w1_copy(0).start()
    for j in range(3, n_tile):
        w2_copy(j).start()
        if j < RING:
            w1_copy(j - 2).start()
    dg_ref[...] = jnp.zeros_like(dg_ref)

    def ahead(m, j):
        @pl.when(m == 0)
        def _():
            w2_copy(j).wait()

        gp_copy(m * n_tile + j).wait()

    def refill(q):
        w1_copy(q).wait()

        @pl.when(q + RING - 2 < total)
        def _():
            w1_copy(q + RING - 2).start()

    def more_slopes(q):
        @pl.when(q < total)
        def _():
            gp_copy(q).start()

    def hidden(m, j, slot, side, keep):
        dact = dot_nt(w2b[j], recv[m])
        da = (gpb[lax.rem(m * n_tile + j, 4)] * dact.T).astype(BF16)
        dob[slot, side] = da
        keep[...] = da

    def run(m):
        @pl.when(stage == last)
        def _():
            for k in range(n_micro):
                @pl.when(m == k)
                def _():
                    top_copy(k).wait()

        @pl.when(stage < last)
        def _():
            next_copy(m).wait_recv()

        save_copy(m).start()
        h_copy(m).start()

        @pl.when(m == 1)
        def _():
            peer_copy(0).start()

        @pl.when(m > 0)
        def _():
            peer_copy(m).start()

        k0 = m * n_pair
        ahead(m, 0)

        @pl.when(k0 >= 2)
        def _():
            da_copy(m, 0, lax.rem(k0, 2), 0).wait()

        acc[...] = jnp.zeros_like(acc)
        hidden(m, 0, lax.rem(k0, 2), 0, da_a)
        da_copy(m, 0, lax.rem(k0, 2), 0).start()
        more_slopes(m * n_tile + 4)

        @pl.loop(1, n_pair)
        def _(k):
            slot = lax.rem(k0 + k, 2)
            j = 2 * k
            q = m * n_tile + j
            ahead(m, j - 1)
            ahead(m, j)
            refill(q - 2)
            refill(q - 1)

            @pl.when(k0 + k >= 2)
            def _():
                da_copy(m, j, slot, 0).wait()

            @pl.when(k0 + k >= 3)
            def _():
                da_copy(m, j, slot, 1).wait()

            hidden(m, j - 1, slot, 1, da_b)
            acc[...] += dot_nt(w1b[lax.rem(q - 2, RING)], da_a)
            hidden(m, j, slot, 0, da_a)
            acc[...] += dot_nt(w1b[lax.rem(q - 1, RING)], da_b)
            da_copy(m, j - 1, slot, 1).start()
            da_copy(m, j, slot, 0).start()
            more_slopes(q + 3)
            more_slopes(q + 4)

        slot = lax.rem(k0 + n_pair, 2)
        q = m * n_tile + n_tile - 1
        ahead(m, n_tile - 1)
        refill(q - 1)
        refill(q)

        @pl.when(k0 + n_pair >= 3)
        def _():
            da_copy(m, 0, slot, 1).wait()

        hidden(m, n_tile - 1, slot, 1, da_b)
        acc[...] += dot_nt(w1b[lax.rem(q - 1, RING)], da_a)
        acc[...] += dot_nt(w1b[lax.rem(q, RING)], da_b)
        da_copy(m, n_tile - 1, slot, 1).start()
        more_slopes(q + 4)

    def finish(m):
        h_copy(m).wait()

        @pl.when((stage > 0) & (m >= 2))
        def _():
            next_copy(m).wait_send()

        @pl.when((stage == 0) & (m >= 1))
        def _():
            for copy in x_copies(m):
                copy.wait()

        @pl.loop(0, d, step=LANES)
        def _(c):
            cols = pl.ds(pl.multiple_of(c, LANES), LANES)
            xbuf[:, cols] = acc[cols, :].T

        oslot = lax.rem(m, 2)

        def norm_rows(i, dg):
            rows = pl.ds(pl.multiple_of(i * 16, 16), 16)
            r = hbuf[rows, :].astype(F32)
            inv = lax.rsqrt(jnp.mean(r * r, axis=-1, keepdims=True) + NORM_EPS)
            hat = r * inv
            dn = xbuf[rows, :]
            dg = dg + jnp.sum((dn * hat).reshape(2, 8, dn.shape[1]), axis=0)
            dgn = dn * g_ref[...]
            grad = recv[m, rows, :].astype(F32) + inv * (dgn - hat * jnp.mean(dgn * hat, axis=-1, keepdims=True))
            obuf[oslot, rows, :] = grad.astype(BF16)
            xbuf[rows, :] = grad
            return dg

        dg_ref[...] += lax.fori_loop(0, n_rows // 16, norm_rows, jnp.zeros(dg_ref.shape, F32))

        @pl.when(m == 0)
        def _():
            pl.semaphore_wait(barrier, 1 + jnp.minimum(stage, 1) + jnp.minimum(last - stage, 1))

        @pl.when(stage > 0)
        def _():
            next_copy(m).start()

        @pl.when(stage == 0)
        def _():
            for copy in x_copies(m):
                copy.start()

    @pl.loop(0, n_micro + 1)
    def _(m):
        @pl.when(m > 0)
        def _():
            finish(m - 1)

        @pl.when(m < n_micro)
        def _():
            run(m)


    for side in range(2):
        for slot in range(2):
            da_copy(0, 0, slot, side).wait()
    for m in range(n_micro):
        save_copy(m).wait()
        peer_copy(m).wait()

    @pl.when(stage > 0)
    def _():
        next_copy(n_micro - 2).wait_send()
        next_copy(n_micro - 1).wait_send()

    @pl.when(stage == 0)
    def _():
        for copy in x_copies(n_micro - 1):
            copy.wait()


def backward(n_stage, tops, hin, gain, w1, w2, gp):
    n_micro, n_tok, d = hin.shape
    f = w1.shape[1]
    n_tile = f // FB
    dma = pltpu.SemaphoreType.DMA
    act = jax.ShapeDtypeStruct(hin.shape, BF16)
    vmem = pl.BlockSpec(memory_space=pltpu.VMEM)
    return pl.pallas_call(
        functools.partial(bwd_kernel, n_stage, n_micro, n_tile),
        out_shape=(act, act,
                   jax.ShapeDtypeStruct((n_tile, n_micro, n_tok, FB), BF16),
                   jax.ShapeDtypeStruct((n_stage, n_micro, n_tok, d // n_stage), F32),
                   jax.ShapeDtypeStruct((8, d), F32)),
        in_specs=[ANY, ANY, ANY, vmem, ANY, ANY, ANY],
        out_specs=(ANY, ANY, ANY, ANY, vmem),
        scratch_shapes=[
            pltpu.VMEM((n_micro, n_tok, d), BF16),
            pltpu.VMEM((2, n_tok, d), BF16),
            pltpu.VMEM((n_tok, d), BF16),
            pltpu.VMEM((d, n_tok), F32),
            pltpu.VMEM((n_tok, d), F32),
            pltpu.VMEM((RING, d, FB), BF16),
            pltpu.VMEM((n_tile, FB, d), BF16),
            pltpu.VMEM((4, n_tok, FB), F32),
            pltpu.VMEM((2, 2, n_tok, FB), BF16),
            pltpu.VMEM((n_tok, FB), BF16),
            pltpu.VMEM((n_tok, FB), BF16),
            dma((n_micro,)), dma((RING,)), dma((n_tile,)), dma((4,)), dma((2, 2)), dma, dma((n_micro,)), dma((n_stage,)),
            dma((2,)), dma((n_micro,)), dma((n_micro,)), dma((n_micro,)),
        ],
        compiler_params=params(1),
        cost_estimate=cost(4 * n_micro * n_tok * d * f, 4 * d * f * (1 + n_micro)),
        name='backward',
    )(*tops, hin, gain, w1, w2, gp)


def logits_kernel(base_ref, h_ref, w_ref, lab_ref, z_ref, st_ref, m_s, s_s, t_s, zs):
    i = pl.program_id(0)

    @pl.when(i == 0)
    def _():
        m_s[...] = jnp.full(m_s.shape, -jnp.inf, F32)
        s_s[...] = jnp.zeros(s_s.shape, F32)
        t_s[...] = jnp.zeros(t_s.shape, F32)
        zs[...] = jnp.full(zs.shape, -jnp.inf, F32)

    def count(z, first):
        lane = lax.broadcasted_iota(jnp.int32, (1, LANES), 1) + first
        cols = [z[:, c:c + LANES] for c in range(0, VB, LANES)]
        m_old = m_s[...]
        m_new = m_old
        for part in cols:
            m_new = jnp.maximum(m_new, part)
        m_ref = jnp.where(m_new == -jnp.inf, 0.0, m_new)
        s_new = s_s[...] * jnp.exp(m_old - m_ref)
        t_new = t_s[...]
        lab = lab_ref[...]
        for c, part in enumerate(cols):
            s_new = s_new + jnp.exp(part - m_ref)
            t_new = t_new + jnp.where(lab == lane + c * LANES, part, 0.0)
        m_s[...] = m_new
        s_s[...] = s_new
        t_s[...] = t_new

    first = base_ref[0] + i * (2 * VB)
    z_ref[0] = dot_nt(h_ref, w_ref[:VB, :])
    count(zs[...], jnp.where(i == 0, -(1 << 20), first - VB))
    z = dot_nt(h_ref, w_ref[VB:, :])
    z_ref[1] = z
    zs[...] = z
    count(z_ref[0], first)

    @pl.when(i == pl.num_programs(0) - 1)
    def _():
        count(zs[...], first + VB)
        m_all = jnp.max(m_s[...], axis=1, keepdims=True)
        s_all = jnp.sum(s_s[...] * jnp.exp(m_s[...] - m_all), axis=1, keepdims=True)
        t_all = jnp.sum(t_s[...], axis=1, keepdims=True)
        col = lax.broadcasted_iota(jnp.int32, m_s.shape, 1)
        packed = jnp.where(col == 0, m_all, jnp.where(col == 1, s_all, t_all))
        st_ref[...] = packed.T[:8]


def logits(base, h, w, lab):
    n_tok, d = h.shape
    n_voc = w.shape[0]
    n_tile = n_voc // VB
    once = pl.Buffered(1)
    return pl.pallas_call(
        logits_kernel,
        out_shape=(jax.ShapeDtypeStruct((n_tile, n_tok, VB), F32), jax.ShapeDtypeStruct((8, n_tok), F32)),
        grid_spec=pltpu.PrefetchScalarGridSpec(
            num_scalar_prefetch=1,
            grid=(n_tile // 2,),
            in_specs=[
                pl.BlockSpec((n_tok, d), home, pipeline_mode=once),
                pl.BlockSpec((2 * VB, d), lambda i, s: (i, 0)),
                pl.BlockSpec((n_tok, LANES), home, pipeline_mode=once),
            ],
            out_specs=(pl.BlockSpec((2, n_tok, VB), lambda i, s: (i, 0, 0)), pl.BlockSpec((8, n_tok), home)),
            scratch_shapes=[pltpu.VMEM((n_tok, LANES), F32)] * 3 + [pltpu.VMEM((n_tok, VB), F32)],
        ),
        compiler_params=params(),
        cost_estimate=cost(2 * n_tok * d * n_voc, 2 * d * n_voc + 4 * n_tok * n_voc),
        name='logits',
    )(base, h, w, lab)


def dz_of(z, lse, lab, lane, scale):
    parts = []
    for c in range(0, z.shape[1], LANES):
        p = jnp.exp(z[:, c:c + LANES] - lse)
        hot = jnp.where(lab == lane + c, 1.0, 0.0)
        parts.append(((p - hot) * scale).astype(BF16))
    return jnp.concatenate(parts, axis=1)


def dhid_kernel(scale, base_ref, z_ref, wa_ref, wb_ref, wl_ref, lse_ref, lab_ref, dz_ref, dh_ref, dz_a, dz_b):
    i = pl.program_id(0)

    @pl.when(i == 0)
    def _():
        dh_ref[...] = jnp.zeros(dh_ref.shape, F32)
        dz_b[...] = jnp.zeros(dz_b.shape, BF16)

    def turn(k, keep):
        lane = lax.broadcasted_iota(jnp.int32, (1, LANES), 1) + (base_ref[0] + (2 * i + k) * VB)
        dz = dz_of(z_ref[k], lse_ref[...], lab_ref[...], lane, scale)
        dz_ref[k] = dz
        keep[...] = dz

    turn(0, dz_a)
    dh_ref[...] += dot_nn(dz_b, wb_ref)
    turn(1, dz_b)
    dh_ref[...] += dot_nn(dz_a, wa_ref)

    @pl.when(i == pl.num_programs(0) - 1)
    def _():
        dh_ref[...] += dot_nn(dz_b, wl_ref)


def dhid(scale, half, n_half, base, z, w, lse, lab):
    n_tile, n_tok, _ = z.shape
    rows = n_tok // n_half
    n_voc, d = w.shape
    once = pl.Buffered(1)
    return pl.pallas_call(
        functools.partial(dhid_kernel, scale),
        out_shape=(jax.ShapeDtypeStruct((n_tile, rows, VB), BF16), jax.ShapeDtypeStruct((rows, d), F32)),
        grid_spec=pltpu.PrefetchScalarGridSpec(
            num_scalar_prefetch=1,
            grid=(n_tile // 2,),
            in_specs=[
                pl.BlockSpec((2, rows, VB), lambda i, s: (i, half, 0)),
                pl.BlockSpec((VB, d), lambda i, s: (2 * i, 0)),
                pl.BlockSpec((VB, d), lambda i, s: (jnp.maximum(2 * i - 1, 0), 0)),
                pl.BlockSpec((VB, d), lambda i, s: (n_tile - 1, 0), pipeline_mode=once),
                pl.BlockSpec((rows, LANES), lambda i, s: (half, 0), pipeline_mode=once),
                pl.BlockSpec((rows, LANES), lambda i, s: (half, 0), pipeline_mode=once),
            ],
            out_specs=(pl.BlockSpec((2, rows, VB), lambda i, s: (i, 0, 0)), pl.BlockSpec((rows, d), home)),
            scratch_shapes=[pltpu.VMEM((rows, VB), BF16)] * 2,
        ),
        compiler_params=params(),
        cost_estimate=cost(2 * rows * d * n_voc, 2 * d * n_voc + 6 * rows * n_voc),
    )(base, z, w, w, w, lse, lab)


def dwout_kernel(scale, s_ref, w_ref, dz0_ref, dz1_ref, ho_ref, hp_ref, lse_ref, lab_ref, *rest):
    out_ref = rest[-1]
    i = pl.program_id(0)

    @pl.when(i < s_ref[2])
    def _():
        rows = dz0_ref.shape[1]
        zp = dot_nt(hp_ref, w_ref)
        own = dot_tn(dz0_ref[0], ho_ref[:rows, :]) + dot_tn(dz1_ref[0], ho_ref[rows:, :])
        lane = lax.broadcasted_iota(jnp.int32, (1, LANES), 1) + (s_ref[0] + (s_ref[1] + i) * VB)
        dzp = dz_of(zp, lse_ref[...], lab_ref[...], lane, scale)
        out_ref[...] = own + dot_tn(dzp, hp_ref)


def dwout(scale, n_step, scalars, w, dz0, dz1, ho, hp, lse, lab, out=None):
    n_voc, d = w.shape
    n_tok = ho.shape[0]
    rows = dz0.shape[1]
    once = pl.Buffered(1)

    def at(i, s):
        return jnp.minimum(s[1] + jnp.minimum(i, jnp.maximum(s[2] - 1, 0)), n_voc // VB - 1)

    more = [] if out is None else [out]
    return pl.pallas_call(
        functools.partial(dwout_kernel, scale),
        out_shape=jax.ShapeDtypeStruct((n_voc, d), F32),
        grid_spec=pltpu.PrefetchScalarGridSpec(
            num_scalar_prefetch=1,
            grid=(n_step,),
            in_specs=[
                pl.BlockSpec((VB, d), lambda i, s: (at(i, s), 0)),
                pl.BlockSpec((1, rows, VB), lambda i, s: (at(i, s), 0, 0)),
                pl.BlockSpec((1, rows, VB), lambda i, s: (at(i, s), 0, 0)),
                pl.BlockSpec((n_tok, d), home, pipeline_mode=once),
                pl.BlockSpec((n_tok, d), home, pipeline_mode=once),
                pl.BlockSpec((n_tok, LANES), home, pipeline_mode=once),
                pl.BlockSpec((n_tok, LANES), home, pipeline_mode=once),
            ] + [ANY] * len(more),
            out_specs=pl.BlockSpec((VB, d), lambda i, s: (at(i, s), 0)),
        ),
        input_output_aliases={} if out is None else {8: 0},
        compiler_params=params(),
        cost_estimate=cost(6 * n_tok * d * n_step * VB, (2 * d + 4 * d + 2 * n_tok) * n_step * VB),
        name='dwout_first' if out is None else 'dwout_rest',
    )(scalars, w, dz0, dz1, ho, hp, lse, lab, *more)


def wgrad_kernel(g_ref, ho_ref, hp_ref, dyo_ref, dyp_ref, w1_ref, w2_ref, u_ref, da_ref, dw1_ref, dw2_ref, nt_s, np_s):
    i = pl.program_id(0)
    n_tok = ho_ref.shape[0]

    @pl.when(i == 0)
    def _():
        def prep(src, base, keep):
            @pl.loop(0, n_tok, step=LANES)
            def _(k):
                rows = pl.ds(pl.multiple_of(k, LANES), LANES)
                r = src[rows, :].astype(F32)
                inv = lax.rsqrt(jnp.mean(r * r, axis=-1, keepdims=True) + NORM_EPS)
                n = (r * inv * g_ref[...]).astype(BF16)
                if keep:
                    np_s[rows, :] = n
                nt_s[:, pl.ds(pl.multiple_of(base + k, LANES), LANES)] = n.T

        prep(ho_ref, 0, False)
        prep(hp_ref, n_tok, True)

    n_col = w1_ref.shape[1]
    a = dot_nn(np_s, w1_ref)
    dact = dot_nt(dyp_ref, w2_ref)
    u_own = u_ref[0].reshape(n_tok, n_col)
    da_own = da_ref[0].reshape(n_tok, n_col)
    dw2_own = dot_tn(u_own, dyo_ref)
    u, slope = gelu_and_slope(a)
    da = (slope * dact).astype(BF16)
    dw1_ref[...] = dot_nn(nt_s[:, :n_tok], da_own) + dot_nn(nt_s[:, n_tok:], da)
    dw2_ref[...] = dw2_own + dot_tn(u.astype(BF16), dyp_ref)


def wgrad(gain, ho, hp, dyo, dyp, w1, w2, u, da):
    n_tok, d = ho.shape
    f = w1.shape[1]
    per = FB // WB
    n_micro, n_row = u.shape[1:3]
    once = pl.Buffered(1)
    full = pl.BlockSpec((n_tok, d), home, pipeline_mode=once)
    act = pl.BlockSpec((1, n_micro, n_row, WB), lambda i: (i // per, 0, 0, i % per))
    return pl.pallas_call(
        wgrad_kernel,
        out_shape=(jax.ShapeDtypeStruct((d, f), F32), jax.ShapeDtypeStruct((f, d), F32)),
        grid=(f // WB,),
        in_specs=[
            pl.BlockSpec((1, d), home, pipeline_mode=once),
            full, full, full, full,
            pl.BlockSpec((d, WB), lambda i: (0, i)),
            pl.BlockSpec((WB, d), lambda i: (i, 0)),
            act, act,
        ],
        out_specs=(pl.BlockSpec((d, WB), lambda i: (0, i)), pl.BlockSpec((WB, d), lambda i: (i, 0))),
        scratch_shapes=[pltpu.VMEM((d, 2 * n_tok), BF16), pltpu.VMEM((n_tok, d), BF16)],
        compiler_params=params(),
        cost_estimate=cost(12 * n_tok * d * f, 12 * d * f + 4 * n_tok * f),
        name='wgrad',
    )(gain, ho, hp, dyo, dyp, w1, w2, u, da)


FIRST_TILES = (21, 18, 12, 9)


def solution(mesh):
    n_stage = mesh.shape['stage']
    n_dp = mesh.shape['dp']
    swap = [(0, 1), (1, 0)]

    def device_step(x_emb, labels, norm_gain, w_up, w_down, w_out):
        n_micro, n_tok, d = x_emb.shape
        own = n_micro * n_tok
        n_voc = w_out.shape[0]
        n_vtile = n_voc // VB
        stage = lax.axis_index('stage')
        dp = lax.axis_index('dp')
        scale = 1.0 / (own * n_dp)
        gain, w1, w2 = norm_gain[0], w_up[0, 0], w_down[0, 0]
        base = (stage * n_voc).reshape(1).astype(jnp.int32)

        def lanes(v):
            return jnp.broadcast_to(v.reshape(own, 1), (own, LANES))

        lab = labels.reshape(own)
        lab_o, lab_p = lanes(lab), lanes(lax.ppermute(lab, 'dp', swap))

        hin, hinp, hfin, gp, u = forward(n_stage, x_emb, gain, w1, w2)
        ho = hfin.reshape(own, d)
        hp = lax.ppermute(ho, 'dp', swap)
        z, stats = logits(base, ho, w_out, lab_o)

        every = lax.all_gather(stats, ('dp', 'stage')).reshape(n_dp, n_stage, 8, own)
        top = jnp.max(every[:, :, 0], axis=1)
        lse = top + jnp.log(jnp.sum(every[:, :, 1] * jnp.exp(every[:, :, 0] - top[:, None]), axis=1))
        loss = jnp.sum(lse - jnp.sum(every[:, :, 2], axis=1)) * scale
        lse_o = lanes(lax.dynamic_index_in_dim(lse, dp, 0, keepdims=False))
        lse_p = lanes(lax.dynamic_index_in_dim(lse, 1 - dp, 0, keepdims=False))

        dzs, tops = [], []
        for half in range(2):
            dz, dh = dhid(scale, half, 2, base, z, w_out, lse_o, lab_o)
            dh = dh + lax.ppermute(dh, 'stage', [(0, 1), (2, 3)])
            dh = dh + lax.ppermute(dh, 'stage', [(1, 3)])
            dzs.append(dz)
            tops.append(dh.astype(BF16).reshape(n_micro // 2, n_tok, d))

        first = jnp.asarray(FIRST_TILES, jnp.int32)[stage].reshape(1)
        s_first = jnp.concatenate([base, jnp.zeros((1,), jnp.int32), first])
        s_rest = jnp.concatenate([base, first, n_vtile - first])
        head = (w_out, dzs[0], dzs[1], ho, hp, lse_p, lab_p)
        gw = dwout(scale, max(FIRST_TILES), s_first, *head)

        tops, gw = lax.optimization_barrier((tops, gw))
        dyin, dyp, da, gx, dg = backward(n_stage, tops, hin, gain, w1, w2, gp)
        gw, dyin = lax.optimization_barrier((gw, dyin))
        gw = dwout(scale, n_vtile - min(FIRST_TILES), s_rest, *head, out=gw)

        gw, gx, dg, dyin = lax.optimization_barrier((gw, gx, dg, dyin))
        dw1, dw2 = wgrad(gain, hin.reshape(own, d), hinp.reshape(own, d), dyin.reshape(own, d), dyp.reshape(own, d), w1, w2, u, da)

        dg = jnp.sum(dg, axis=0)
        dg = dg + lax.ppermute(dg, 'dp', swap)
        grad_x = jnp.where(stage == 0, gx[0], 0.0)
        for k in range(1, n_stage):
            grad_x = grad_x + lax.ppermute(gx[k], 'stage', [(0, k)])
        return loss.reshape(1), grad_x, dg.reshape(1, 1, d), dw1[None, None], dw2[None, None], gw

    tok_spec = ('pod', 'dp')
    stage_spec = ('pod', 'stage')
    rows = P(stage_spec)
    toks = P(None, tok_spec)
    in_specs = (toks, toks, rows, rows, rows, rows)
    out_specs = (P('pod'), P(*toks, 'stage'), rows, rows, rows, rows)
    return jax.shard_map(device_step, mesh=mesh, in_specs=in_specs, out_specs=out_specs, check_vma=False)
```

time: 1090 us -> 1080 us (level)
  no operation moved by 1% of the time
where the time goes in v2:
time: 1080 us; the launch traced here: 1070 us
  Pallas kernels  920 us (85%)
  waiting for transfers between devices  63.7 us (6%)
  other arithmetic  34.5 us (3%)
  starting transfers between devices  28.6 us (3%)
  blocking collectives  13.7 us (1%)
  local copies, waits for them, and re-layouts  11 us (1%)
    pallas_call x1, Pallas kernels, wgrad(): pl.pallas_call(wgrad_kernel, out_shape=(jax.ShapeDtypeStruct((d, f), F32)...  242 us
    pallas_call x1, Pallas kernels, forward(): pl.pallas_call(functools.partial(fwd_kernel, n_stage, n_micro, n_tile), o...  215 us
    pallas_call x2, Pallas kernels, dwout(): pl.pallas_call(functools.partial(dwout_kernel, scale), out_shape=jax.Shap...  186 us
    pallas_call x1, Pallas kernels, backward(): pl.pallas_call(functools.partial(bwd_kernel, n_stage, n_micro, n_tile), o...  131 us
    pallas_call x2, Pallas kernels, dhid(): pl.pallas_call(functools.partial(dhid_kernel, scale), out_shape=(jax.Shap...  83.9 us
    ppermute x1, waiting for transfers between devices, device_step(): lab_o, lab_p = (lanes(lab), lanes(lax.ppermute(lab, 'dp', swap)))  63.6 us
    pallas_call x1, Pallas kernels, logits(): pl.pallas_call(logits_kernel, out_shape=(jax.ShapeDtypeStruct((n_tile, n_...  62.7 us
  transfers between devices with their start and end apart: 10, of which 1 were waited for; matrix products, arithmetic and copies ran while one was open for 3% of the time, Pallas kernels for 41%

profile of v2, /device:TPU:0, one launch (start us, length us, event | category | flops | bytes accessed | tf_op | source)
XLA Modules:
  0.0 1075.0 jit_solution(5221067650028887298)
XLA Ops:
  0.6 0.7 copy.18
  1.3 0.0 copy-start.1
  1.3 214.8 %forward.1 = (bf16[4,256,2048]{2,1,0:T(8,128)(2,1)}, bf16[4,256,2048]{2,1,0:T(8,128)(2,1)}, bf16[4,256,2048]{2,1,0:T(8,128)(2,1)}, f32[4,16,256,512]{3,2,1,0:T(8,128)}, bf16[16,4,256,512]{3,2,1,0:T(8,128)(2,1)}) custom-call(bf16[4,256,2048]{2,1,0:T(8,128)(2,1)} %x_ref.1, f32[1,2048]{1,0:T(1,128)} %bitcast.63, bf16[2048,8192]{1,0:T(8,128)(2,1)} %bitcast.53, ...), custom_call_target="tpu_custom_call" | custom-call | flops 68719476736 | bytes 335544320 | tf_op jit(solution)/shard_map/forward/pallas_call | solution.py:278
  216.1 0.0 copy-done.1
  216.2 1.0 broadcast_in_dim.38.lab_ref
  217.2 62.7 %logits.1 = (f32[24,1024,512]{2,1,0:T(8,128)}, f32[8,1024]{1,0:T(8,128)}) custom-call(s32[1]{0:T(128)} %bitcast.base_ref, bf16[1024,2048]{1,0:T(8,128)(2,1)} %bitcast.59, bf16[12288,2048]{1,0:T(8,128)(2,1)} %w_ref.5, s32[1024,128]{1,0:T(8,128)} %broadcast_in_dim.38.lab_ref), custom_call_target="tpu_custom_call" | custom-call | flops 51539607552 | bytes 100663296 | tf_op jit(solution)/shard_map/logits/pallas_call | solution.py:650
  279.9 13.7 %all-gather = f32[64,1024]{1,0:T(8,128)S(1)} all-gather(f32[8,1024]{1,0:T(8,128)} %get-tuple-element.34), channel_id=2, replica_groups=mesh['pod'=1,'dp'=2,'stage'=4] {'dp','stage'}, dimensions={0}, use_global_device_ids=true | all-gather | bytes 294912 | tf_op jit(solution)/shard_map/all_gather | solution.py:867
  293.6 0.1 slice_reduce_fusion
  293.8 0.7 subtract_reduce_fusion
  294.5 1.0 broadcast_in_dim.40.lse_ref
  295.5 42.0 %shard_map.119 = (bf16[24,512,512]{2,1,0:T(8,128)(2,1)}, f32[512,2048]{1,0:T(8,128)}) custom-call(s32[1]{0:T(128)} %bitcast.base_ref, f32[24,1024,512]{2,1,0:T(8,128)} %get-tuple-element.35.z_ref, bf16[12288,2048]{1,0:T(8,128)(2,1)} %w_ref.5, bf16[12288,2048]{1,0:T(8,128)(2,1)} %w_ref.5, bf16[12288,2048]{1,0:T(8,128)(2,1)} %w_ref.5, ...), custom_call_target="tpu_custom_call" | custom-call | flops 25769803776 | bytes 88080384 | tf_op jit(solution)/shard_map/pallas_call | solution.py:708
  337.5 0.0 copy-start.2
  337.5 0.0 copy-start.3
  337.5 3.4 collective-permute-start.4
  340.9 41.9 %shard_map.118 = (bf16[24,512,512]{2,1,0:T(8,128)(2,1)}, f32[512,2048]{1,0:T(8,128)}) custom-call(s32[1]{0:T(128)} %bitcast.base_ref, f32[24,1024,512]{2,1,0:T(8,128)} %get-tuple-element.35.z_ref, bf16[12288,2048]{1,0:T(8,128)(2,1)} %w_ref.5, bf16[12288,2048]{1,0:T(8,128)(2,1)} %w_ref.5, bf16[12288,2048]{1,0:T(8,128)(2,1)} %w_ref.5, ...), custom_call_target="tpu_custom_call" | custom-call | flops 25769803776 | bytes 88080384 | tf_op jit(solution)/shard_map/pallas_call | solution.py:708
  382.8 3.3 collective-permute-start.2
  386.2 1.3 collective-permute-start
  387.4 0.0 copy-done.2
  387.4 0.7 collective-permute-start.1
  388.2 0.0 copy-done.3
  388.2 0.6 dynamic_slice.10
  389.4 1.3 pad_add_fusion.s_ref
  390.7 1.2 pad_add_fusion.1.s_ref
  392.6 0.0 copy-start
  392.6 0.0 collective-permute-done.4
  392.6 6.7 add.44
  399.3 2.6 collective-permute-start.5
  401.9 0.0 collective-permute-done.2
  401.9 0.0 copy-done
  401.9 5.0 add.42
  406.9 2.9 collective-permute-start.3
  409.8 63.6 %collective-permute-done.1 = s32[1024]{0:T(1024)S(1)} collective-permute-done((s32[1024]{0:T(1024)S(1)}, s32[1024]{0:T(1024)S(1)}, u32[]{:S(2)}, u32[]{:S(2)}) %collective-permute-start.1) | collective-permute-done | bytes 4128 | tf_op jit(solution)/shard_map/ppermute | solution.py:860
  473.4 0.0 collective-permute-done.hp_ref
  473.4 1.0 broadcast_in_dim.43.lab_ref
  474.4 1.0 broadcast_in_dim.42.lse_ref
  475.4 156.0 %dwout_first.1.rest_0_ = f32[12288,2048]{1,0:T(8,128)} custom-call(s32[3]{0:T(128)} %pad_add_fusion.1.s_ref, bf16[12288,2048]{1,0:T(8,128)(2,1)} %w_ref.5, bf16[24,512,512]{2,1,0:T(8,128)(2,1)} %get-tuple-element.36.dz0_ref, bf16[24,512,512]{2,1,0:T(8,128)(2,1)} %get-tuple-element.37.dz1_ref, bf16[1024,2048]{1,0:T(8,128)(2,1)} %bitcast.61, ...), custom_call_target="tpu_custom_call" | custom-call | flops 135291469824 | bytes 154140672 | tf_op jit(solution)/shard_map/dwout_first/pallas_call | solution.py:754
  631.4 0.0 collective-permute-done.5
  631.4 5.4 add_convert_fusion
  636.9 0.0 collective-permute-done.3
  636.9 5.4 add_convert_fusion.1
  642.3 131.1 %backward.1 = (bf16[4,256,2048]{2,1,0:T(8,128)(2,1)}, bf16[4,256,2048]{2,1,0:T(8,128)(2,1)}, bf16[16,4,256,512]{3,2,1,0:T(8,128)(2,1)}, f32[4,4,256,512]{3,2,1,0:T(8,128)}, f32[8,2048]{1,0:T(8,128)}) custom-call(bf16[2,256,2048]{2,1,0:T(8,128)(2,1)} %bitcast.45, bf16[2,256,2048]{2,1,0:T(8,128)(2,1)} %bitcast.44, ...), custom_call_target="tpu_custom_call" | custom-call | flops 68719476736 | bytes 335544320 | tf_op jit(solution)/shard_map/backward/pallas_call | solution.py:569
  773.4 29.6 %dwout_rest.1 = f32[12288,2048]{1,0:T(8,128)} custom-call(s32[3]{0:T(128)} %pad_add_fusion.s_ref, bf16[12288,2048]{1,0:T(8,128)(2,1)} %w_ref.5, bf16[24,512,512]{2,1,0:T(8,128)(2,1)} %get-tuple-element.36.dz0_ref, bf16[24,512,512]{2,1,0:T(8,128)(2,1)} %get-tuple-element.37.dz1_ref, bf16[1024,2048]{1,0:T(8,128)(2,1)} %bitcast.62, ...), custom_call_target="tpu_custom_call", output_to_operand_aliasing={{}: (8, {})} | custom-call | flops 96636764160 | bytes 110100480 | tf_op jit(solution)/shard_map/dwout_rest/pallas_call | solution.py:754
  803.0 1.5 reduce_sum.39
  804.5 1.8 collective-permute-start.9
  806.2 5.7 slice_bitcast_fusion.2
  811.9 2.6 collective-permute-start.6
  814.5 2.6 collective-permute-start.8
  817.2 7.3 collective-permute-start.7
  824.4 242.0 %wgrad.1 = (f32[2048,8192]{1,0:T(8,128)}, f32[8192,2048]{1,0:T(8,128)}) custom-call(f32[1,2048]{1,0:T(1,128)} %bitcast.65, bf16[1024,2048]{1,0:T(8,128)(2,1)} %bitcast.66, bf16[1024,2048]{1,0:T(8,128)(2,1)} %bitcast.67, bf16[1024,2048]{1,0:T(8,128)(2,1)} %bitcast.68, bf16[1024,2048]{1,0:T(8,128)(2,1)} %bitcast.69, bf16[2048,8192]{1,0:T(8,128)(2,1)} %bitcast.55, ...), custom_call_target="tpu_custom_call" | custom-call | flops 206158430208 | bytes 234881024 | tf_op jit(solution)/shard_map/wgrad/pallas_call | solution.py:818
  1066.4 0.0 collective-permute-done.9
  1066.4 1.3 add.49
  1067.7 0.0 collective-permute-done.6
  1067.7 0.0 collective-permute-done.8
  1067.7 0.0 collective-permute-done.7
  1067.7 5.9 fusion.1
  (2 shorter events, 0.1 us)
Async XLA Ops:
  1.3 214.8 %copy-start.1 = (s32[1,2,4,128]{3,1,2,0:T(2,128)}, s32[1,2,4,128]{3,1,2,0:T(2,128)S(1)}, u32[]{:S(2)}) copy-start(s32[1,2,4,128]{3,1,2,0:T(2,128)S(1)} %copy.18) | copy-start | bytes 12292
  337.5 49.9 %copy-start.2 = (s32[1,2,4,128]{3,1,2,0:T(2,128)S(1)}, s32[1,2,4,128]{3,1,2,0:T(2,128)}, u32[]{:S(2)}) copy-start(s32[1,2,4,128]{3,1,2,0:T(2,128)} %copy-done.1) | copy-start | bytes 12292
  337.5 50.7 %copy-start.3 = (s32[4]{0:T(128)S(1)}, s32[4]{0:T(128)}, u32[]{:S(2)}) copy-start(s32[4]{0:T(128)} %constant.38.clone) | copy-start | bytes 52
  337.5 55.1 %collective-permute-start.4 = (f32[512,2048]{1,0:T(8,128)}, f32[512,2048]{1,0:T(8,128)}, u32[]{:S(2)}, u32[]{:S(2)}) collective-permute-start(f32[512,2048]{1,0:T(8,128)} %get-tuple-element.39), channel_id=1, source_target_pairs={{0,1},{2,3},{4,5},{6,7}} | collective-permute-start | bytes 12582920 | tf_op jit(solution)/shard_map/ppermute | solution.py:877
  382.8 19.1 %collective-permute-start.2 = (f32[512,2048]{1,0:T(8,128)}, f32[512,2048]{1,0:T(8,128)}, u32[]{:S(2)}, u32[]{:S(2)}) collective-permute-start(f32[512,2048]{1,0:T(8,128)} %get-tuple-element.38), channel_id=1, source_target_pairs={{0,1},{2,3},{4,5},{6,7}} | collective-permute-start | bytes 12582920 | tf_op jit(solution)/shard_map/ppermute | solution.py:877
  386.2 87.3 %collective-permute-start = (bf16[1024,2048]{1,0:T(8,128)(2,1)}, bf16[1024,2048]{1,0:T(8,128)(2,1)}, u32[]{:S(2)}, u32[]{:S(2)}) collective-permute-start(bf16[1024,2048]{1,0:T(8,128)(2,1)} %bitcast.60), channel_id=1, source_target_pairs={{0,4},{4,0},{1,5},{5,1},{2,6},{6,2},{3,7},{7,3}} | collective-permute-start | bytes 12582920 | tf_op jit(solution)/shard_map/ppermute | solution.py:864
  387.4 86.0 %collective-permute-start.1 = (s32[1024]{0:T(1024)S(1)}, s32[1024]{0:T(1024)S(1)}, u32[]{:S(2)}, u32[]{:S(2)}) collective-permute-start(s32[1024]{0:T(1024)S(1)} %bitcast.50), channel_id=1, source_target_pairs={{0,4},{4,0},{1,5},{5,1},{2,6},{6,2},{3,7},{7,3}} | collective-permute-start | bytes 12296 | tf_op jit(solution)/shard_map/ppermute | solution.py:860
  392.6 9.3 copy-start
  399.3 232.2 %collective-permute-start.5 = (f32[512,2048]{1,0:T(8,128)}, f32[512,2048]{1,0:T(8,128)}, u32[]{:S(2)}, u32[]{:S(2)}) collective-permute-start(f32[512,2048]{1,0:T(8,128)} %add.44), channel_id=1, source_target_pairs={{1,3},{5,7}} | collective-permute-start | bytes 12582920 | tf_op jit(solution)/shard_map/ppermute | solution.py:878
  406.9 230.0 %collective-permute-start.3 = (f32[512,2048]{1,0:T(8,128)}, f32[512,2048]{1,0:T(8,128)}, u32[]{:S(2)}, u32[]{:S(2)}) collective-permute-start(f32[512,2048]{1,0:T(8,128)} %add.42), channel_id=1, source_target_pairs={{1,3},{5,7}} | collective-permute-start | bytes 12582920 | tf_op jit(solution)/shard_map/ppermute | solution.py:878
  804.5 262.0 %collective-permute-start.9 = (f32[2048]{0:T(1024)}, f32[2048]{0:T(1024)}, u32[]{:S(2)}, u32[]{:S(2)}) collective-permute-start(f32[2048]{0:T(1024)} %reduce_sum.39), channel_id=1, source_target_pairs={{0,4},{4,0},{1,5},{5,1},{2,6},{6,2},{3,7},{7,3}} | collective-permute-start | bytes 24584 | tf_op jit(solution)/shard_map/ppermute | solution.py:897
  811.9 255.8 %collective-permute-start.6 = (f32[4,256,512]{2,1,0:T(8,128)}, f32[4,256,512]{2,1,0:T(8,128)}, u32[]{:S(2)}, u32[]{:S(2)}) collective-permute-start(f32[4,256,512]{2,1,0:T(8,128)} %get-tuple-element.64), channel_id=1, source_target_pairs={{0,1},{4,5}} | collective-permute-start | bytes 6291464 | tf_op jit(solution)/shard_map/ppermute | solution.py:900
  814.5 253.2 %collective-permute-start.8 = (f32[4,256,512]{2,1,0:T(8,128)}, f32[4,256,512]{2,1,0:T(8,128)}, u32[]{:S(2)}, u32[]{:S(2)}) collective-permute-start(f32[4,256,512]{2,1,0:T(8,128)} %get-tuple-element.65), channel_id=1, source_target_pairs={{0,3},{4,7}} | collective-permute-start | bytes 6291464 | tf_op jit(solution)/shard_map/ppermute | solution.py:900
  817.2 250.6 %collective-permute-start.7 = (f32[4,256,512]{2,1,0:T(8,128)}, f32[4,256,512]{2,1,0:T(8,128)}, u32[]{:S(2)}, u32[]{:S(2)}) collective-permute-start(f32[4,256,512]{2,1,0:T(8,128)} %get-tuple-element.66), channel_id=1, source_target_pairs={{0,2},{4,6}} | collective-permute-start | bytes 6291464 | tf_op jit(solution)/shard_map/ppermute | solution.py:900
